TPU v7x, 16 devices: a whole 2x2x2 slice. The times are simulated.
16 devices in a mesh: col: 2 (over z), row: 8 (over y, x, core).
Axes of the slice: x: 2, y: 2, z: 2, core: 2. Of those that a mesh axis runs over, the one named last changes fastest.
Arguments:
- vel_x: float32 [16, 2, 1024, 512], P(None, None, 'row', 'col')
- vel_y: float32 [16, 2, 1024, 512], P(None, None, 'row', 'col')
- pot_temp: float32 [16, 2, 1024, 512], P(None, None, 'row', 'col')
- salinity: float32 [16, 2, 1024, 512], P(None, None, 'row', 'col')
- surf_eta: float32 [2, 1024, 512], P(None, 'row', 'col')
- trans_x: float32 [2, 1024, 512], P(None, 'row', 'col')
- trans_y: float32 [2, 1024, 512], P(None, 'row', 'col')
- col_depth: float32 [1024, 512], P('row', 'col')
- wet_levels: int32 [1024, 512], P('row', 'col')
- avg_weights: float32 [30], replicated
Outputs:
- output 1: float32 [2, 1024, 512], P(None, 'row', 'col')
- output 2: float32 [2, 1024, 512], P(None, 'row', 'col')
- output 3: float32 [2, 1024, 512], P(None, 'row', 'col')
- output 4: float32 [16, 2, 1024, 512], P(None, None, 'row', 'col')
- output 5: float32 [16, 2, 1024, 512], P(None, None, 'row', 'col')
- output 6: float32 [16, 2, 1024, 512], P(None, None, 'row', 'col')
- output 7: float32 [16, 2, 1024, 512], P(None, None, 'row', 'col')
All inputs are finite; a program needn't handle non-finite values.
Results may differ from a plain program's by a relative error of at most 0.001.
Values sent between devices are 32-bit elements.
A program may use at most 1 GiB of HBM per device.

v0:
```python
import functools
import jax
import jax.numpy as jnp
from jax import lax
from jax.sharding import PartitionSpec as P

WAVE_COURANT = 0.4
THERM_EXP = 0.2
HALINE_CON = 0.15
PRESS_SCALE = 0.5
VISC_NUMBER = 1.0
DIFF_NUMBER = 0.5


def take_east(field_in, col_count):
    edge_slab = field_in[..., :1]
    received = lax.ppermute(edge_slab, "col", [(source, (source - 1) % col_count) for source in range(col_count)])
    return jnp.concatenate([field_in[..., 1:], received], axis=-1)


def take_west(field_in, col_count):
    edge_slab = field_in[..., -1:]
    received = lax.ppermute(edge_slab, "col", [(source, (source + 1) % col_count) for source in range(col_count)])
    return jnp.concatenate([received, field_in[..., :-1]], axis=-1)


def take_north(field_in, row_count):
    edge_slab = field_in[..., :1, :]
    received = lax.ppermute(edge_slab, "row", [(source, source - 1) for source in range(1, row_count)])
    return jnp.concatenate([field_in[..., 1:, :], received], axis=-2)


def take_south(field_in, row_count):
    edge_slab = field_in[..., -1:, :]
    received = lax.ppermute(edge_slab, "row", [(source, source + 1) for source in range(row_count - 1)])
    return jnp.concatenate([received, field_in[..., :-1, :]], axis=-2)


def vertical_solve(right_side, face_mask, strength):
    mask_below = jnp.concatenate([face_mask[1:], jnp.zeros_like(face_mask[:1])], axis=0)
    face_up = face_mask * mask_below
    face_down = jnp.concatenate([jnp.zeros_like(face_up[:1]), face_up[:-1]], axis=0)
    lower_diag = -strength * face_down
    upper_diag = -strength * face_up
    main_diag = 1.0 + strength * (face_down + face_up)

    def forward(state_prev, level_row):
        upper_prev, side_prev = state_prev
        low_k, diag_k, up_k, side_k = level_row
        divisor = diag_k - low_k * upper_prev
        upper_new = up_k / divisor
        side_new = (side_k - low_k * side_prev) / divisor
        return (upper_new, side_new), (upper_new, side_new)

    zero_level = jnp.zeros_like(right_side[0])
    upper_all, side_all = lax.scan(forward, (zero_level, zero_level), (lower_diag, main_diag, upper_diag, right_side))[1]

    def backward(sol_next, level_row):
        up_k, side_k = level_row
        sol_k = side_k - up_k * sol_next
        return sol_k, sol_k

    return lax.scan(backward, zero_level, (upper_all, side_all), reverse=True)[1]


def three_d_step(vel_x, vel_y, pot_temp, salinity, col_depth, wet_levels, shift_east, shift_west, shift_north, shift_south):
    level_count = vel_x.shape[0]
    levels = jnp.arange(level_count).reshape(level_count, 1, 1, 1)
    cell_mask = (levels < wet_levels).astype(jnp.float32)
    xface_mask = cell_mask * (levels < shift_east(wet_levels)).astype(jnp.float32)
    yface_mask = cell_mask * (levels < shift_north(wet_levels)).astype(jnp.float32)
    density = HALINE_CON * salinity - THERM_EXP * pot_temp
    pressure = (PRESS_SCALE / level_count) * (jnp.cumsum(density, axis=0) - 0.5 * density)
    vy_south = shift_south(vel_y)
    vx_north = shift_north(vel_x)
    vy_at_x = 0.25 * (vel_y + vy_south + shift_east(vel_y) + shift_east(vy_south))
    vx_at_y = 0.25 * (vel_x + shift_west(vel_x) + vx_north + shift_west(vx_north))
    tend_x = xface_mask * (pressure - shift_east(pressure) - 0.5 * vel_x * (shift_east(vel_x) - shift_west(vel_x)) - 0.5 * vy_at_x * (vx_north - shift_south(vel_x)))
    tend_y = yface_mask * (pressure - shift_north(pressure) - 0.5 * vx_at_y * (shift_east(vel_y) - shift_west(vel_y)) - 0.5 * vel_y * (shift_north(vel_y) - vy_south))
    count_x = jnp.maximum(jnp.sum(xface_mask, axis=0), 1.0)
    count_y = jnp.maximum(jnp.sum(yface_mask, axis=0), 1.0)
    depth_x = 0.5 * (col_depth + shift_east(col_depth)) * xface_mask[0]
    depth_y = 0.5 * (col_depth + shift_north(col_depth)) * yface_mask[0]
    force_x = depth_x * jnp.sum(tend_x, axis=0) / count_x
    force_y = depth_y * jnp.sum(tend_y, axis=0) / count_y
    pred_x = vertical_solve(vel_x + tend_x, xface_mask, VISC_NUMBER)
    pred_y = vertical_solve(vel_y + tend_y, yface_mask, VISC_NUMBER)
    dev_x = pred_x - jnp.sum(pred_x, axis=0) / count_x
    dev_y = pred_y - jnp.sum(pred_y, axis=0) / count_y

    def tracer_step(tracer):
        flux_x = vel_x * 0.5 * (tracer + shift_east(tracer))
        flux_y = vel_y * 0.5 * (tracer + shift_north(tracer))
        advected = cell_mask * (tracer - (flux_x - shift_west(flux_x) + flux_y - shift_south(flux_y)))
        return vertical_solve(advected, cell_mask, DIFF_NUMBER)

    return cell_mask[0], xface_mask, yface_mask, depth_x, depth_y, force_x, force_y, dev_x, dev_y, tracer_step(pot_temp), tracer_step(salinity)


def barotropic(surf_eta, trans_x, trans_y, force_x, force_y, depth_x, depth_y, wet_top, xface_top, yface_top, avg_weights, shift_east, shift_west, shift_north, shift_south):
    sub_count = avg_weights.shape[0]
    step_x = force_x / sub_count
    step_y = force_y / sub_count

    def subcycle(sub_state, weight):
        eta_now, tx_now, ty_now, eta_avg, tx_avg, ty_avg = sub_state
        eta_now = wet_top * (eta_now - WAVE_COURANT * (tx_now - shift_west(tx_now) + ty_now - shift_south(ty_now)))
        tx_now = xface_top * (tx_now + step_x - WAVE_COURANT * depth_x * (shift_east(eta_now) - eta_now))
        ty_now = yface_top * (ty_now + step_y - WAVE_COURANT * depth_y * (shift_north(eta_now) - eta_now))
        return (eta_now, tx_now, ty_now, eta_avg + weight * eta_now, tx_avg + weight * tx_now, ty_avg + weight * ty_now), None

    zero_field = jnp.zeros_like(surf_eta)
    end_state = lax.scan(subcycle, (surf_eta, trans_x, trans_y, zero_field, zero_field, zero_field), avg_weights)[0]
    return end_state[3], end_state[4], end_state[5]


def solution(mesh):
    col_count = mesh.shape["col"]
    row_count = mesh.shape["row"]
    shift_east = functools.partial(take_east, col_count=col_count)
    shift_west = functools.partial(take_west, col_count=col_count)
    shift_north = functools.partial(take_north, row_count=row_count)
    shift_south = functools.partial(take_south, row_count=row_count)

    def local_step(vel_x, vel_y, pot_temp, salinity, surf_eta, trans_x, trans_y, col_depth, wet_levels, avg_weights):
        wet_top, xface_mask, yface_mask, depth_x, depth_y, force_x, force_y, dev_x, dev_y, temp_new, salt_new = three_d_step(vel_x, vel_y, pot_temp, salinity, col_depth, wet_levels, shift_east, shift_west, shift_north, shift_south)
        eta_new, trans_x_new, trans_y_new = barotropic(surf_eta, trans_x, trans_y, force_x, force_y, depth_x, depth_y, wet_top, xface_mask[0], yface_mask[0], avg_weights, shift_east, shift_west, shift_north, shift_south)
        vel_x_new = xface_mask * (dev_x + trans_x_new / (depth_x + 1.0 - xface_mask[0]))
        vel_y_new = yface_mask * (dev_y + trans_y_new / (depth_y + 1.0 - yface_mask[0]))
        return eta_new, trans_x_new, trans_y_new, vel_x_new, vel_y_new, temp_new, salt_new

    spec_3d = P(None, None, "row", "col")
    spec_2d = P(None, "row", "col")
    spec_map = P("row", "col")
    spec_weights = P()
    return jax.shard_map(local_step, mesh=mesh, in_specs=(spec_3d, spec_3d, spec_3d, spec_3d, spec_2d, spec_2d, spec_2d, spec_map, spec_map, spec_weights), out_specs=(spec_2d, spec_2d, spec_2d, spec_3d, spec_3d, spec_3d, spec_3d), check_vma=False)
```

profile of v0, /device:TPU:0, one launch (start us, length us, event | category | flops | bytes accessed | tf_op | source)
XLA Modules:
  0.0 1316.4 jit_solution(205173307834436403)
XLA Ops:
  15.9 8.2 fusion.97
  24.2 10.1 subtract_multiply_fusion
  34.3 4.9 slice.283
  41.1 7.3 fusion.92
  111.0 5.1 multiply_add_fusion
  156.1 4.9 fusion.27
  170.4 7.3 collective-permute-start.13
  178.0 21.0 %fusion.47 = (f32[16,2,128,256]{3,2,1,0:T(8,128)}, f32[16,2,128,256]{3,2,1,0:T(8,128)}, f32[16,2,128,256]{3,2,1,0:T(8,128)}, f32[16,2,128,256]{3,2,1,0:T(8,128)}) fusion(f32[16,2,128,256]{3,2,1,0:T(8,128)} %param.31, f32[16,2,128,1]{3,2,1,0:T(8,128)} %copy.36, f32[16,2,128,255]{3,2,1,0:T(8,128)} %slice.254, f32[16,2,128,256]{3,2,1,0:T(8,128)} %param.28, ...), kind=kLoop, calls=%fused_computation.115 | loop fusion | flops 14680064 | bytes 50331648 | tf_op jit(solution)/shard_map/mul | solution.py:92
  225.9 21.7 %fusion.86 = (f32[16,2,128,256]{3,2,1,0:T(8,128)}, f32[16,2,128,256]{3,2,1,0:T(8,128)}) fusion(f32[16,2,128,256]{3,2,1,0:T(8,128)} %param.29, f32[16,2,127,256]{3,2,1,0:T(8,128)} %get-tuple-element.1160, f32[16,2,1,256]{3,2,1,0:T(1,128)S(1)} %collective-permute-done.9, f32[16,2,1,256]{3,2,1,0:T(1,128)S(1)} %collective-permute-done.19, ...), kind=kLoop, calls=%fused_computation.181 | loop fusion | flops 23068672 | bytes 56623104 | tf_op jit(solution)/shard_map/add | solution.py:87
  252.6 65.6 %while.160 = (s32[]{:T(128)}, f32[2,128,256]{2,1,0:T(8,128)}, f32[2,128,256]{2,1,0:T(8,128)}, f32[16,2,128,256]{3,2,1,0:T(8,128)}, f32[16,2,128,256]{3,2,1,0:T(8...) while((s32[]{:T(128)}, f32[2,128,256]{2,1,0:T(8,128)}, ...), condition=%wide.region_13.14_spmd.clone, body=%wide.region_12.13_spmd.clone.sunk | while | flops 524291 | bytes 3015295 | solution.py:56
  320.7 31.2 %while.161 = (s32[]{:T(128)}, f32[2,128,256]{2,1,0:T(8,128)S(1)}, f32[16,2,128,256]{3,2,1,0:T(8,128)}, f32[16,2,128,256]{3,2,1,0:T(8,128)}, f32[16,2,128,256]{3,...) while((s32[]{:T(128)}, f32[2,128,256]{2,1,0:T(8,128)S(1)}, f32[16,2,128,256]{3,2,1,0:T(8,128)}, ...), condition=%wide.region_15.16_spmd.clone, body=%wide.region_14.15_spmd.clone.sunk | while | flops 196612 | bytes 1310831 | solution.py:63
  357.9 22.4 %fusion.89 = (f32[16,2,128,256]{3,2,1,0:T(8,128)}, f32[16,2,128,256]{3,2,1,0:T(8,128)}) fusion(f32[16,2,128,256]{3,2,1,0:T(8,128)} %param.28, f32[16,2,127,256]{3,2,1,0:T(8,128)} %get-tuple-element.1168, f32[16,2,1,256]{3,2,1,0:T(1,128)S(1)} %collective-permute-done.13, f32[16,2,1,256]{3,2,1,0:T(1,128)} %collective-permute-done.12, ...), kind=kLoop, calls=%fused_computation.182 | loop fusion | flops 23068672 | bytes 56623104 | tf_op jit(solution)/shard_map/add | solution.py:86
  385.4 61.7 %while.158 = (s32[]{:T(128)}, f32[2,128,256]{2,1,0:T(8,128)S(1)}, f32[2,128,256]{2,1,0:T(8,128)S(1)}, f32[16,2,128,256]{3,2,1,0:T(8,128)}, f32[16,2,128,256]{3,2...) while((s32[]{:T(128)}, f32[2,128,256]{2,1,0:T(8,128)S(1)}, ...), condition=%wide.region_8.9_spmd.clone, body=%wide.region_7.8_spmd.clone.sunk | while | flops 524291 | bytes 3015295 | solution.py:56
  449.5 31.2 %while.159 = (s32[]{:T(128)}, f32[2,128,256]{2,1,0:T(8,128)S(1)}, f32[16,2,128,256]{3,2,1,0:T(8,128)}, f32[16,2,128,256]{3,2,1,0:T(8,128)}, f32[16,2,128,256]{3,...) while((s32[]{:T(128)}, f32[2,128,256]{2,1,0:T(8,128)S(1)}, f32[16,2,128,256]{3,2,1,0:T(8,128)}, ...), condition=%wide.region_10.11_spmd.clone, body=%wide.region_9.10_spmd.clone.sunk | while | flops 196612 | bytes 1310831 | solution.py:63
  493.5 583.3 %while.157 = (s32[]{:T(128)}, f32[2,128,256]{2,1,0:T(8,128)S(1)}, f32[2,128,256]{2,1,0:T(8,128)S(1)}, f32[2,128,256]{2,1,0:T(8,128)S(1)}, f32[2,128,256]{2,1,0:T...) while((s32[]{:T(128)}, f32[2,128,256]{2,1,0:T(8,128)S(1)}, ...), condition=%wide.region_6.7_spmd.clone, body=%wide.region_5.6_spmd.clone.sunk | while | flops 1966083 | bytes 7764316 | solution.py:113
  498.1 4.8 collective-permute-done.1
  539.6 4.6 collective-permute-done.1
  578.8 4.4 collective-permute-done.1
  617.5 4.4 collective-permute-done.1
  656.1 4.4 collective-permute-done.1
  694.7 4.4 collective-permute-done.1
  733.3 4.4 collective-permute-done.1
  771.9 4.4 collective-permute-done.1
  810.5 4.4 collective-permute-done.1
  1003.6 4.4 collective-permute-done.1
  1042.2 4.4 collective-permute-done.1
  1080.3 5.1 add_multiply_fusion
  1093.9 20.9 %fusion.51 = (f32[16,2,128,256]{3,2,1,0:T(8,128)}, f32[16,2,128,256]{3,2,1,0:T(8,128)}) fusion(f32[16,2,128,256]{3,2,1,0:T(8,128)} %param.31, f32[16,2,128,256]{3,2,1,0:T(8,128)} %get-tuple-element.1154, f32[16,2,128,256]{3,2,1,0:T(8,128)} %get-tuple-element.1151, f32[16,2,128,255]{3,2,1,0:T(8,128)} %bitcast.178, f32[16,2,128,1]{3,2,1,0:T(8,128)} %copy.38, ...), kind=kLoop, calls=%fused_computation.120 | loop fusion | flops 14680064 | bytes 52428800 | tf_op jit(solution)/shard_map/mul | solution.py:94
  1119.8 61.8 %while.164 = (s32[]{:T(128)}, f32[2,128,256]{2,1,0:T(8,128)S(1)}, f32[2,128,256]{2,1,0:T(8,128)S(1)}, f32[16,2,128,256]{3,2,1,0:T(8,128)}, f32[16,2,128,256]{3,2...) while((s32[]{:T(128)}, f32[2,128,256]{2,1,0:T(8,128)S(1)}, ...), condition=%wide.region_22.23_spmd.clone, body=%wide.region_21.22_spmd.clone.sunk | while | flops 524291 | bytes 3015295 | solution.py:56
  1184.0 31.2 %while.165 = (s32[]{:T(128)}, f32[2,128,256]{2,1,0:T(8,128)S(1)}, f32[16,2,128,256]{3,2,1,0:T(8,128)}, f32[16,2,128,256]{3,2,1,0:T(8,128)}, f32[16,2,128,256]{3,...) while((s32[]{:T(128)}, f32[2,128,256]{2,1,0:T(8,128)S(1)}, f32[16,2,128,256]{3,2,1,0:T(8,128)}, ...), condition=%wide.region_24.25_spmd.clone, body=%wide.region_23.24_spmd.clone.sunk | while | flops 196612 | bytes 1310831 | solution.py:63
  1220.3 62.0 %while.162 = (s32[]{:T(128)}, f32[2,128,256]{2,1,0:T(8,128)S(1)}, f32[2,128,256]{2,1,0:T(8,128)S(1)}, f32[16,2,128,256]{3,2,1,0:T(8,128)}, f32[16,2,128,256]{3,2...) while((s32[]{:T(128)}, f32[2,128,256]{2,1,0:T(8,128)S(1)}, ...), condition=%wide.region_18.19_spmd.clone, body=%wide.region_17.18_spmd.clone.sunk | while | flops 524291 | bytes 3015295 | solution.py:56
  1284.9 31.2 %while.163 = (s32[]{:T(128)}, f32[2,128,256]{2,1,0:T(8,128)S(1)}, f32[16,2,128,256]{3,2,1,0:T(8,128)}, f32[16,2,128,256]{3,2,1,0:T(8,128)}, f32[16,2,128,256]{3,...) while((s32[]{:T(128)}, f32[2,128,256]{2,1,0:T(8,128)S(1)}, f32[16,2,128,256]{3,2,1,0:T(8,128)}, ...), condition=%wide.region_20.21_spmd.clone, body=%wide.region_19.20_spmd.clone.sunk | while | flops 196612 | bytes 1310831 | solution.py:63
  (1022 shorter events, 1125.2 us)
Async XLA Ops:
  2.3 153.7 %collective-permute-start.12 = (f32[16,2,1,256]{3,2,1,0:T(1,128)}, f32[16,2,1,256]{3,2,1,0:T(1,128)}, u32[]{:S(2)}, u32[]{:S(2)}) collective-permute-start(f32[16,2,1,256]{3,2,1,0:T(1,128)} %get-tuple-element.1169), channel_id=1, source_target_pairs={{1,0},{2,1},{3,2},{4,3},{5,4},{6,5},{7,6},{9,8},{10,9},{11,10},{12... | collective-permute-start | bytes 98312 | tf_op jit(solution)/shard_map/ppermute | solution.py:29
  4.5 103.0 %collective-permute-start.4 = (s32[128,1]{1,0:T(8,128)S(1)}, s32[128,1]{1,0:T(8,128)}, u32[]{:S(2)}, u32[]{:S(2)}) collective-permute-start(s32[128,1]{1,0:T(8,128)S(1)} %slice.207), channel_id=1, source_target_pairs={{0,8},{8,0},{1,9},{9,1},{2,10},{10,2},{3,11},{11,3},{4,12},{12,4},... | collective-permute-start | bytes 1544 | tf_op jit(solution)/shard_map/ppermute | solution.py:17
  9.1 101.2 %collective-permute-start.14 = (s32[1,256]{1,0:T(1,128)}, s32[1,256]{1,0:T(1,128)}, u32[]{:S(2)}, u32[]{:S(2)}) collective-permute-start(s32[1,256]{1,0:T(1,128)} %slice.228), channel_id=1, source_target_pairs={{1,0},{2,1},{3,2},{4,3},{5,4},{6,5},{7,6},{9,8},{10,9},{11,10},{12... | collective-permute-start | bytes 3080 | tf_op jit(solution)/shard_map/ppermute | solution.py:29
  15.9 115.8 %collective-permute-start.8 = (f32[16,2,128,1]{2,0,3,1:T(8,128)}, f32[16,2,128,1]{2,0,3,1:T(8,128)S(1)}, u32[]{:S(2)}, u32[]{:S(2)}) collective-permute-start(f32[16,2,128,1]{2,0,3,1:T(8,128)} %copy.40), channel_id=1, source_target_pairs={{0,8},{8,0},{1,9},{9,1},{2,10},{10,2},{3,11},{11,3},{4,12},{12,4},... | collective-permute-start | bytes 49160 | tf_op jit(solution)/shard_map/ppermute | solution.py:23
  105.5 22.7 %collective-permute-start.5 = (f32[128,1]{1,0:T(8,128)}, f32[128,1]{1,0:T(8,128)S(1)}, u32[]{:S(2)}, u32[]{:S(2)}) collective-permute-start(f32[128,1]{1,0:T(8,128)} %slice.210), channel_id=1, source_target_pairs={{0,8},{8,0},{1,9},{9,1},{2,10},{10,2},{3,11},{11,3},{4,12},{12,4},... | collective-permute-start | bytes 1544 | tf_op jit(solution)/shard_map/ppermute | solution.py:17
  108.4 21.7 %collective-permute-start.15 = (f32[1,256]{1,0:T(1,128)}, f32[1,256]{1,0:T(1,128)S(1)}, u32[]{:S(2)}, u32[]{:S(2)}) collective-permute-start(f32[1,256]{1,0:T(1,128)} %slice.231), channel_id=1, source_target_pairs={{1,0},{2,1},{3,2},{4,3},{5,4},{6,5},{7,6},{9,8},{10,9},{11,10},{12... | collective-permute-start | bytes 3080 | tf_op jit(solution)/shard_map/ppermute | solution.py:29
  131.7 9.4 collective-permute-start.6
  131.7 12.6 collective-permute-start.7
  133.7 15.8 %collective-permute-start.20 = (f32[16,2,128,1]{2,0,3,1:T(8,128)}, f32[16,2,128,1]{2,0,3,1:T(8,128)S(1)}, u32[]{:S(2)}, u32[]{:S(2)}) collective-permute-start(f32[16,2,128,1]{2,0,3,1:T(8,128)} %copy.43), channel_id=1, source_target_pairs={{0,8},{8,0},{1,9},{9,1},{2,10},{10,2},{3,11},{11,3},{4,12},{12,4},... | collective-permute-start | bytes 49160 | tf_op jit(solution)/shard_map/ppermute | solution.py:17
  133.8 19.0 %collective-permute-start.24 = (f32[16,2,128,1]{2,0,3,1:T(8,128)}, f32[16,2,128,1]{2,0,3,1:T(8,128)S(1)}, u32[]{:S(2)}, u32[]{:S(2)}) collective-permute-start(f32[16,2,128,1]{2,0,3,1:T(8,128)} %copy.44), channel_id=1, source_target_pairs={{0,8},{8,0},{1,9},{9,1},{2,10},{10,2},{3,11},{11,3},{4,12},{12,4},... | collective-permute-start | bytes 49160 | tf_op jit(solution)/shard_map/ppermute | solution.py:17
  143.1 81.1 %collective-permute-start.16 = (f32[16,2,1,256]{3,2,1,0:T(1,128)S(1)}, f32[16,2,1,256]{3,2,1,0:T(1,128)S(1)}, u32[]{:S(2)}, u32[]{:S(2)}) collective-permute-start(f32[16,2,1,256]{3,2,1,0:T(1,128)S(1)} %copy-done.32), channel_id=1, source_target_pairs={{1,0},{2,1},{3,2},{4,3},{5,4},{6,5},{7,6},{9,8},{10,9},{11,10},{12... | collective-permute-start | bytes 98312 | tf_op jit(solution)/shard_map/ppermute | solution.py:29
  146.5 15.8 %collective-permute-start.9 = (f32[16,2,1,256]{3,2,1,0:T(1,128)S(1)}, f32[16,2,1,256]{3,2,1,0:T(1,128)S(1)}, u32[]{:S(2)}, u32[]{:S(2)}) collective-permute-start(f32[16,2,1,256]{3,2,1,0:T(1,128)S(1)} %copy-done.36), channel_id=1, source_target_pairs={{0,1},{1,2},{2,3},{3,4},{4,5},{5,6},{6,7},{8,9},{9,10},{10,11},{11... | collective-permute-start | bytes 98312 | tf_op jit(solution)/shard_map/ppermute | solution.py:35
  151.5 74.4 %collective-permute-start.19 = (f32[16,2,1,256]{3,2,1,0:T(1,128)S(1)}, f32[16,2,1,256]{3,2,1,0:T(1,128)S(1)}, u32[]{:S(2)}, u32[]{:S(2)}) collective-permute-start(f32[16,2,1,256]{3,2,1,0:T(1,128)S(1)} %copy-done.35), channel_id=1, source_target_pairs={{1,0},{2,1},{3,2},{4,3},{5,4},{6,5},{7,6},{9,8},{10,9},{11,10},{12... | collective-permute-start | bytes 98312 | tf_op jit(solution)/shard_map/ppermute | solution.py:29
  154.7 22.9 %collective-permute-start.22 = (f32[16,2,1,256]{3,2,1,0:T(1,128)S(1)}, f32[16,2,1,256]{3,2,1,0:T(1,128)S(1)}, u32[]{:S(2)}, u32[]{:S(2)}) collective-permute-start(f32[16,2,1,256]{3,2,1,0:T(1,128)S(1)} %copy-done.34), channel_id=1, source_target_pairs={{1,0},{2,1},{3,2},{4,3},{5,4},{6,5},{7,6},{9,8},{10,9},{11,10},{12... | collective-permute-start | bytes 98312 | tf_op jit(solution)/shard_map/ppermute | solution.py:29
  161.0 17.0 %collective-permute-start.26 = (f32[16,2,1,256]{3,2,1,0:T(1,128)S(1)}, f32[16,2,1,256]{3,2,1,0:T(1,128)S(1)}, u32[]{:S(2)}, u32[]{:S(2)}) collective-permute-start(f32[16,2,1,256]{3,2,1,0:T(1,128)S(1)} %copy-done.33), channel_id=1, source_target_pairs={{1,0},{2,1},{3,2},{4,3},{5,4},{6,5},{7,6},{9,8},{10,9},{11,10},{12... | collective-permute-start | bytes 98312 | tf_op jit(solution)/shard_map/ppermute | solution.py:29
  170.4 187.6 %collective-permute-start.13 = (f32[16,2,1,256]{3,2,1,0:T(1,128)}, f32[16,2,1,256]{3,2,1,0:T(1,128)S(1)}, u32[]{:S(2)}, u32[]{:S(2)}) collective-permute-start(f32[16,2,1,256]{3,2,1,0:T(1,128)} %get-tuple-element.1170), channel_id=1, source_target_pairs={{0,1},{1,2},{2,3},{3,4},{4,5},{5,6},{6,7},{8,9},{9,10},{10,11},{11... | collective-permute-start | bytes 98312 | tf_op jit(solution)/shard_map/ppermute | solution.py:35
  177.7 44.2 %collective-permute-start.17 = (f32[16,2,128,1]{2,0,3,1:T(8,128)S(1)}, f32[16,2,128,1]{2,0,3,1:T(8,128)S(1)}, u32[]{:S(2)}, u32[]{:S(2)}) collective-permute-start(f32[16,2,128,1]{2,0,3,1:T(8,128)S(1)} %copy.27), channel_id=1, source_target_pairs={{0,8},{8,0},{1,9},{9,1},{2,10},{10,2},{3,11},{11,3},{4,12},{12,4},... | collective-permute-start | bytes 49160 | tf_op jit(solution)/shard_map/ppermute | solution.py:23
  220.2 135.1 %collective-permute-start.11 = (f32[16,2,128,1]{2,0,3,1:T(8,128)S(1)}, f32[16,2,128,1]{2,0,3,1:T(8,128)}, u32[]{:S(2)}, u32[]{:S(2)}) collective-permute-start(f32[16,2,128,1]{2,0,3,1:T(8,128)S(1)} %copy.25), channel_id=1, source_target_pairs={{0,8},{8,0},{1,9},{9,1},{2,10},{10,2},{3,11},{11,3},{4,12},{12,4},... | collective-permute-start | bytes 49160 | tf_op jit(solution)/shard_map/ppermute | solution.py:17
  223.8 864.5 %collective-permute-start.21 = (f32[16,2,128,1]{2,0,3,1:T(8,128)}, f32[16,2,128,1]{2,0,3,1:T(8,128)}, u32[]{:S(2)}, u32[]{:S(2)}) collective-permute-start(f32[16,2,128,1]{2,0,3,1:T(8,128)} %copy.33), channel_id=1, source_target_pairs={{0,8},{8,0},{1,9},{9,1},{2,10},{10,2},{3,11},{11,3},{4,12},{12,4},... | collective-permute-start | bytes 49160 | tf_op jit(solution)/shard_map/ppermute | solution.py:23
  224.1 867.0 %collective-permute-start.25 = (f32[16,2,128,1]{2,0,3,1:T(8,128)}, f32[16,2,128,1]{2,0,3,1:T(8,128)}, u32[]{:S(2)}, u32[]{:S(2)}) collective-permute-start(f32[16,2,128,1]{2,0,3,1:T(8,128)} %copy.37), channel_id=1, source_target_pairs={{0,8},{8,0},{1,9},{9,1},{2,10},{10,2},{3,11},{11,3},{4,12},{12,4},... | collective-permute-start | bytes 49160 | tf_op jit(solution)/shard_map/ppermute | solution.py:23
  351.9 741.9 %collective-permute-start.23 = (f32[16,2,1,256]{3,2,1,0:T(1,128)}, f32[16,2,1,256]{3,2,1,0:T(1,128)}, u32[]{:S(2)}, u32[]{:S(2)}) collective-permute-start(f32[16,2,1,256]{3,2,1,0:T(1,128)} %slice.297), channel_id=1, source_target_pairs={{0,1},{1,2},{2,3},{3,4},{4,5},{5,6},{6,7},{8,9},{9,10},{10,11},{11... | collective-permute-start | bytes 98312 | tf_op jit(solution)/shard_map/ppermute | solution.py:35
  493.5 9.3 collective-permute-start
  514.6 9.0 collective-permute-start
  535.5 8.7 collective-permute-start
  574.8 8.4 collective-permute-start
  613.4 8.4 collective-permute-start
  652.1 8.4 collective-permute-start
  690.7 8.4 collective-permute-start
  729.3 8.4 collective-permute-start
  767.9 8.4 collective-permute-start
  806.5 8.4 collective-permute-start
  1076.8 17.1 %collective-permute-start.27 = (f32[16,2,1,256]{3,2,1,0:T(1,128)}, f32[16,2,1,256]{3,2,1,0:T(1,128)S(1)}, u32[]{:S(2)}, u32[]{:S(2)}) collective-permute-start(f32[16,2,1,256]{3,2,1,0:T(1,128)} %slice.301), channel_id=1, source_target_pairs={{0,1},{1,2},{2,3},{3,4},{4,5},{5,6},{6,7},{8,9},{9,10},{10,11},{11... | collective-permute-start | bytes 98312 | tf_op jit(solution)/shard_map/ppermute | solution.py:35
  (153 other events, 1455.5 us)
where the time goes:
time: 1330 us; the launch traced here: 1320 us
  other arithmetic  599 us (45%)
  local copies, waits for them, and re-layouts  327 us (25%)
  starting transfers between devices  210 us (16%)
  waiting for transfers between devices  177 us (13%)
    dynamic_update_slice x128, other arithmetic, vertical_solve(): lax.scan(forward, (zero_level, zero_level), (lower_diag, main_diag, upper...  253 us
    ppermute x35, waiting for transfers between devices, take_west(): lax.ppermute(edge_slab, 'col', [(source, (source + 1) % col_count) for so...  126 us
    add x30, other arithmetic, subcycle(): ty_avg + weight * ty_now  86.3 us
    ppermute x34, starting transfers between devices, take_south(): lax.ppermute(edge_slab, 'row', [(source, source + 1) for source in range(...  83.4 us
    add x30, other arithmetic, subcycle(): eta_avg + weight * eta_now  76.7 us
    mul x64, local copies, waits for them, and re-layouts, forward(): divisor = diag_k - low_k * upper_prev  63.1 us
    div x64, local copies, waits for them, and re-layouts, forward(): upper_new = up_k / divisor  58.9 us
    ppermute x38, waiting for transfers between devices, take_east(): lax.ppermute(edge_slab, 'col', [(source, (source - 1) % col_count) for so...  51.6 us
  transfers between devices with their start and end apart: 144, of which 60 were waited for; matrix products, arithmetic and copies ran while one was open for 53% of the time, Pallas kernels for 0%

commit v1 on v0

v1 whole, which is shorter than its diff:
```python
import functools
import jax
import jax.numpy as jnp
from jax import lax
from jax.experimental import pallas as pl
from jax.experimental.pallas import tpu as pltpu
from jax.sharding import PartitionSpec as P

SUB = 8
LANE = 128
LAST = 127
ZERO = 0.0
ONE = 1.0
HALF = 0.5
I0, I1, I2, I3 = range(4)
WAVE = 0.4
THERM = 0.2
HALINE = 0.15
PRESS = HALF
VISC = ONE
DIFF = HALF
LEV = 16
MEM = I2
NSUB = 30
ROWS = LANE
COLS = 256
NR = SUB
NC = I2
HALO = 32
NEXT = 144
EXT = 152
BEXT = 208
NEAR = 192
F32 = jnp.float32
CHUNK = 16
NCH = ROWS // CHUNK
SLOTS = I3
BPC = CHUNK // SUB
MESH = pl.DeviceIdType.MESH
LIMIT = 67043328
TILES = (slice(I0, LANE), slice(LANE, 256))
ANY = pl.BlockSpec(memory_space=pl.ANY)
VM = pl.BlockSpec(memory_space=pltpu.VMEM)
SM = pl.BlockSpec(memory_space=pltpu.SMEM)


def solve_factors(strength):
    gain, inner, last = [], [], []
    prev = None
    for k in range(LEV):
        if k == I0:
            diag, edge = ONE + strength, ONE
        else:
            diag, edge = ONE + 2.0 * strength - strength * prev, ONE + strength - strength * prev
        inner.append(ONE / diag)
        last.append(ONE / edge)
        prev = strength / diag
        gain.append(prev)
    return gain, inner, last


def lane_ids():
    return lax.broadcasted_iota(jnp.int32, (SUB, LANE), I1)


def rot(x, shift):
    shift %= LANE
    return x if shift == I0 else pltpu.roll(x, shift, I1)


def neighbours():
    col = lax.axis_index("col")
    row = lax.axis_index("row")
    other = I1 - col
    north = lax.rem(row + I1, NR)
    south = lax.rem(row + NR - I1, NR)
    return {"x": (other, row), "n": (col, north), "s": (col, south), "nx": (other, north), "sx": (other, south)}


def enter(ids):
    barrier = pltpu.get_barrier_semaphore()
    for target in ids.values():
        pl.semaphore_signal(barrier, inc=I1, device_id=target, device_id_type=MESH)
    pl.semaphore_wait(barrier, len(ids))


def wide_pack(lane, m0t0, m0t1, m1t0, m1t1):
    first = jnp.where(lane < 64, m0t0, m0t1)
    second = jnp.where(lane < 64, m1t0, m1t1)
    return jnp.where((lane < 32) | (lane >= 96), first, rot(second, 64))


def edges_kernel(u, v, te, sa, eta, tx, ty, dep, kmt, px, pd, hr, hx2, hd2, hre, hrx, hry, hrh, hrk, big, s2, sh, sk, pk, rowb, pk2, load_sem, load2_sem, send_sem, recv_sem):
    ids = neighbours()
    fields = (u, v, te, sa)
    loads = []
    for m in range(MEM):
        loads.append([pltpu.make_async_copy(fields[f].at[:, m], big.at[m, f], load_sem.at[m, f]) for f in range(4)])
    loads2 = [pltpu.make_async_copy(a, s2.at[i], load2_sem.at[i]) for i, a in enumerate((eta, tx, ty))]
    loads2.append(pltpu.make_async_copy(dep, sh, load2_sem.at[I3]))
    loads2.append(pltpu.make_async_copy(kmt, sk, load2_sem.at[4]))
    for cp in loads2:
        cp.start()
    for cp in loads[I0] + loads[I1]:
        cp.start()
    enter(ids)
    sent = []

    def send(src, dst, who):
        i = len(sent)
        cp = pltpu.make_async_remote_copy(src_ref=src, dst_ref=dst, send_sem=send_sem.at[i], recv_sem=recv_sem.at[i], device_id=ids[who], device_id_type=MESH)
        cp.start()
        sent.append(cp)

    for src, dst in ((eta, hre), (tx, hrx), (ty, hry)):
        send(src.at[:, pl.ds(ROWS - HALO, HALO), :], dst.at[I0], "n")
        send(src.at[:, pl.ds(I0, HALO), :], dst.at[I1], "s")
    for src, dst in ((dep, hrh), (kmt, hrk)):
        send(src.at[pl.ds(ROWS - HALO, HALO), :], dst.at[I0], "n")
        send(src.at[pl.ds(I0, HALO), :], dst.at[I1], "s")
    lane = lane_ids()
    for cp in loads2:
        cp.wait()

    for r in range(ROWS // SUB):
        rows = pl.ds(SUB * r, SUB)
        for i in range(I3):
            pk2[i, rows, :] = wide_pack(lane, *[s2[i, m, rows, t] for m in range(MEM) for t in TILES])
        pk2[I3, rows, :] = wide_pack(lane, *[sh[rows, t] for t in TILES], *[sk[rows, t].astype(F32) for t in TILES])
    pair = lax.rem(lane + I1, LANE) // I2

    def pack3(m):
        for cp in loads[m]:
            cp.wait()

        def body(g, carry):
            for j in range(4):
                rows = pl.ds(pl.multiple_of(g * 32 + SUB * j, SUB), SUB)
                acc = jnp.zeros((SUB, LANE), F32)
                for f in range(4):
                    for k in range(LEV):
                        q = f * LEV + k
                        both = jnp.where(lane < 64, big[m, f, k, rows, TILES[I0]], big[m, f, k, rows, TILES[I1]])
                        acc = jnp.where(pair == q, rot(both, I2 * q), acc)
                pk[m, rows, :] = acc
            return carry

        lax.fori_loop(I0, 4, body, I0)
        for f in range(4):
            for t in range(I2):
                for g in range(I2):
                    ks = pl.ds(SUB * g, SUB)
                    rowb[I0, m, f, t, ks, :] = big[m, f, ks, ROWS - I1, TILES[t]]
                    rowb[I1, m, f, t, ks, :] = big[m, f, ks, I0, TILES[t]]

    def send3(m):
        send(pk.at[m], px.at[m], "x")
        send(pk.at[m, pl.ds(ROWS - SUB, SUB), :], pd.at[I0, m], "nx")
        send(pk.at[m, pl.ds(I0, SUB), :], pd.at[I1, m], "sx")
        send(rowb.at[I0, m], hr.at[I0, m], "n")
        send(rowb.at[I1, m], hr.at[I1, m], "s")

    send(pk2, hx2, "x")
    send(pk2.at[:, pl.ds(ROWS - HALO, HALO), :], hd2.at[I0], "nx")
    send(pk2.at[:, pl.ds(I0, HALO), :], hd2.at[I1], "sx")
    pack3(I0)
    send3(I0)
    pack3(I1)
    send3(I1)
    for cp in sent:
        cp.wait()


def sds(*shape, dtype=F32):
    return jax.ShapeDtypeStruct(shape, dtype)


NSEND_A = 23


def edges_call(u, v, te, sa, eta, tx, ty, dep, kmt):
    return pl.pallas_call(
        edges_kernel,
        name="edges",
        out_shape=(
            sds(MEM, ROWS, LANE), sds(I2, MEM, SUB, LANE), sds(I2, MEM, 4, I2, LEV, LANE),
            sds(4, ROWS, LANE), sds(I2, 4, HALO, LANE),
            sds(I2, MEM, HALO, COLS), sds(I2, MEM, HALO, COLS), sds(I2, MEM, HALO, COLS),
            sds(I2, HALO, COLS), sds(I2, HALO, COLS, dtype=jnp.int32),
        ),
        in_specs=[ANY] * 9,
        out_specs=(ANY,) * 10,
        scratch_shapes=[
            pltpu.VMEM((MEM, 4, LEV, ROWS, COLS), F32),
            pltpu.VMEM((I3, MEM, ROWS, COLS), F32),
            pltpu.VMEM((ROWS, COLS), F32),
            pltpu.VMEM((ROWS, COLS), jnp.int32),
            pltpu.VMEM((MEM, ROWS, LANE), F32),
            pltpu.VMEM((I2, MEM, 4, I2, LEV, LANE), F32),
            pltpu.VMEM((4, ROWS, LANE), F32),
            pltpu.SemaphoreType.DMA((MEM, 4)),
            pltpu.SemaphoreType.DMA((5,)),
            pltpu.SemaphoreType.DMA((NSEND_A,)),
            pltpu.SemaphoreType.DMA((NSEND_A,)),
        ],
        compiler_params=pltpu.CompilerParams(collective_id=I0, has_side_effects=True, vmem_limit_bytes=LIMIT),
    )(u, v, te, sa, eta, tx, ty, dep, kmt)


def columns_kernel(u, v, te, sa, px, pd, hr, dep, kmt, hx2, hrh, hrk, bu, bv, ot, os, sx, sy, nx, ny, us, vs, ts, ss, ps, vel, uwl, stage, pxs, hrs, hs, ki, kf, hks, obu, obv, ost, oss, load_sem, misc_sem, out_sem):
    row = lax.axis_index("row")
    not_south = jnp.where(row == I0, ZERO, ONE).astype(F32)
    not_north = jnp.where(row == NR - I1, ZERO, ONE).astype(F32)
    fields = ((u, us), (v, vs), (te, ts), (sa, ss))

    def load_copies(c):
        rows = pl.ds(pl.multiple_of(CHUNK * c, CHUNK), CHUNK)
        slot = lax.rem(c, SLOTS)
        return [pltpu.make_async_copy(src.at[:, :, rows, :], stage.at[slot, f], load_sem.at[slot, f]) for f, (src, _) in enumerate(fields)]

    def out_copies(c):
        rows = pl.ds(pl.multiple_of(CHUNK * c, CHUNK), CHUNK)
        return [pltpu.make_async_copy(a.at[:, :, rows, :], b.at[:, :, rows, :], out_sem.at[i]) for i, (a, b) in enumerate(((obu, bu), (obv, bv), (ost, ot), (oss, os)))]

    for c in range(NCH - I1, NCH - I1 - SLOTS, -I1):
        for cp in load_copies(jnp.int32(c)):
            cp.start()
    misc = [
        pltpu.make_async_copy(px, pxs.at[:, pl.ds(SUB, ROWS), :], misc_sem.at[I0]),
        pltpu.make_async_copy(pd.at[I0], pxs.at[:, pl.ds(I0, SUB), :], misc_sem.at[I1]),
        pltpu.make_async_copy(pd.at[I1], pxs.at[:, pl.ds(SUB + ROWS, SUB), :], misc_sem.at[I2]),
        pltpu.make_async_copy(hr, hrs, misc_sem.at[I3]),
        pltpu.make_async_copy(hx2.at[I3], hks, misc_sem.at[4]),
    ]
    for t in range(I2):
        cols = pl.ds(LANE * t, LANE)
        misc.append(pltpu.make_async_copy(dep.at[:, cols], hs.at[t, pl.ds(SUB, ROWS), :], misc_sem.at[5 + 4 * t]))
        misc.append(pltpu.make_async_copy(kmt.at[:, cols], ki.at[t, pl.ds(SUB, ROWS), :], misc_sem.at[6 + 4 * t]))
        misc.append(pltpu.make_async_copy(hrh.at[I1, pl.ds(I0, SUB), cols], hs.at[t, pl.ds(SUB + ROWS, SUB), :], misc_sem.at[7 + 4 * t]))
        misc.append(pltpu.make_async_copy(hrk.at[I1, pl.ds(I0, SUB), cols], ki.at[t, pl.ds(SUB + ROWS, SUB), :], misc_sem.at[SUB + 4 * t]))
    for cp in misc:
        cp.start()
    for cp in misc:
        cp.wait()
    lane = lane_ids()
    is_last = lane == LAST
    is_first = lane == I0
    two = range(I2)
    for m in range(MEM):
        pxs[m, I0:SUB, :] = pxs[m, I0:SUB, :] * not_south
        pxs[m, SUB + ROWS:NEXT, :] = pxs[m, SUB + ROWS:NEXT, :] * not_north
        for f, (_, dst) in enumerate(fields):
            for t in two:
                for g in two:
                    ks = pl.ds(SUB * g, SUB)
                    dst[t, ks, m, 7:SUB, :] = (hrs[I0, m, f, t, ks, :] * not_south)[:, None, :]
                    dst[t, ks, m, SUB + ROWS:9 + ROWS, :] = (hrs[I1, m, f, t, ks, :] * not_north)[:, None, :]
    for t in two:
        kf[t, SUB:SUB + ROWS, :] = ki[t, SUB:SUB + ROWS, :].astype(F32)
        kf[t, SUB + ROWS:NEXT, :] = ki[t, SUB + ROWS:NEXT, :].astype(F32) * not_north
    rho_s = PRESS / LEV * HALINE
    rho_t = PRESS / LEV * THERM
    gain, inner, last = solve_factors(DIFF)
    zero = jnp.zeros((SUB, LANE), F32)

    def east(a, b, halo):
        ra, rb = rot(a, LAST), rot(b, LAST)
        return jnp.where(is_last, rb, ra), jnp.where(is_last, halo, rb)

    def west(a, b, halo):
        ra, rb = rot(a, I1), rot(b, I1)
        return jnp.where(is_first, halo, ra), jnp.where(is_first, ra, rb)

    def keep_east(m, k, rows, a, b, edge):
        for t, x in enumerate(east(a, b, rot(edge, LAST - I2 * (LEV + k)))):
            vel[t, k, m, rows, :] = x

    def unpack(r, m, k, edge):
        slot = lax.rem(jnp.maximum(r, I0) // BPC, SLOTS)
        src_rows = pl.ds(pl.multiple_of(SUB * lax.rem(jnp.maximum(r, I0), BPC), SUB), SUB)
        dst_rows = pl.ds(pl.multiple_of(jnp.where(r < I0, NEXT, SUB * r + SUB), SUB), SUB)
        for f, (_, dst) in enumerate(fields):
            x = [stage[slot, f, k, m, src_rows, TILES[t]] for t in two]
            for t in two:
                dst[t, k, m, dst_rows, :] = x[t]
            if f == I1:
                keep_east(m, k, dst_rows, x[I0], x[I1], edge)

    def prime(m, carry):
        south, north, first = pl.ds(I0, SUB), pl.ds(SUB + ROWS, SUB), pl.ds(ROWS, SUB)
        below = [zero, zero]
        for k in range(LEV):
            unpack(jnp.int32(ROWS // SUB - I1), m, k, pxs[m, first, :])
            keep_east(m, k, south, vs[I0, k, m, south, :], vs[I1, k, m, south, :], pxs[m, south, :])
            for t, x in enumerate(west(us[I0, k, m, north, :], us[I1, k, m, north, :], rot(pxs[m, north, :], 129 - I2 * k))):
                uwl[t, k, m, north, :] = x
            for t in two:
                half = (HALF * rho_s) * ss[t, k, m, north, :] - (HALF * rho_t) * ts[t, k, m, north, :]
                ps[t, k, m, north, :] = below[t] + half
                below[t] = (below[t] + half) + half
        return carry

    def block(r):
        y = pl.multiple_of(r * SUB + SUB, SUB)
        rows = pl.ds(y, SUB)
        up = pl.ds(y + I1, SUB)
        down = pl.ds(y - I1, SUB)
        south = pl.ds(y - SUB, SUB)
        out_rows = pl.ds(pl.multiple_of(r * SUB, SUB), SUB)
        kc = [kf[t, rows, :] for t in two]
        hk = hks[out_rows, :]
        ke = east(kc[I0], kc[I1], rot(hk, 63))
        hc = [hs[t, rows, :] for t in two]
        he = east(hc[I0], hc[I1], rot(hk, LAST))
        kx = [jnp.minimum(kc[t], ke[t]) for t in two]
        ky = [jnp.minimum(kc[t], kf[t, up, :]) for t in two]
        scale_x, scale_y = [], []
        for t in two:
            nx[out_rows, TILES[t]] = kx[t]
            ny[out_rows, TILES[t]] = ky[t]
            scale_x.append(jnp.where(kx[t] > ZERO, HALF * (hc[t] + he[t]), ZERO) / (jnp.maximum(kx[t], ONE) * NSUB))
            scale_y.append(jnp.where(ky[t] > ZERO, HALF * (hc[t] + hs[t, up, :]), ZERO) / (jnp.maximum(ky[t], ONE) * NSUB))

        def member(m, carry):
            pc = pxs[m, rows, :]
            edge = pxs[m, south, :]
            below = [zero, zero, zero]
            sum_x = [zero, zero]
            sum_y = [zero, zero]
            run_t = [None, None]
            run_s = [None, None]
            for k in range(LEV):
                unpack(r - I1, m, k, edge)
                q_u, q_v, q_t, q_s = k, LEV + k, I2 * LEV + k, I3 * LEV + k
                uc = [us[t, k, m, rows, :] for t in two]
                vc = [vs[t, k, m, rows, :] for t in two]
                vd = [vs[t, k, m, down, :] for t in two]
                tc = [ts[t, k, m, rows, :] for t in two]
                sc = [ss[t, k, m, rows, :] for t in two]
                t_east = rot(pc, LAST - I2 * q_t)
                s_east = rot(pc, LAST - I2 * q_s)
                press = []
                for i, (a, b) in enumerate(((tc[I0], sc[I0]), (tc[I1], sc[I1]), (t_east, s_east))):
                    half = (HALF * rho_s) * b - (HALF * rho_t) * a
                    now = below[i] + half
                    below[i] = now + half
                    press.append(now)
                pe = east(press[I0], press[I1], press[I2])
                ue = east(uc[I0], uc[I1], rot(pc, LAST - I2 * q_u))
                uw = west(uc[I0], uc[I1], rot(pc, 129 - I2 * q_u))
                vw = west(vc[I0], vc[I1], rot(pc, 129 - I2 * q_v))
                ve = [vel[t, k, m, rows, :] for t in two]
                for t in two:
                    ps[t, k, m, rows, :] = press[t]
                    uwl[t, k, m, rows, :] = uw[t]
                for t in two:
                    un, ud = us[t, k, m, up, :], us[t, k, m, down, :]
                    vq = (vc[t] + vd[t]) + (ve[t] + vel[t, k, m, down, :])
                    uq = (uc[t] + un) + (uw[t] + uwl[t, k, m, up, :])
                    gu = (press[t] - pe[t]) - HALF * (uc[t] * (ue[t] - uw[t])) - 0.125 * (vq * (un - ud))
                    gu = jnp.where(kx[t] > float(k), gu, ZERO)
                    sum_x[t] = sum_x[t] + gu
                    obu[k, m, out_rows, TILES[t]] = uc[t] + gu
                    gv = (press[t] - ps[t, k, m, up, :]) - 0.125 * (uq * (ve[t] - vw[t])) - HALF * (vc[t] * (vs[t, k, m, up, :] - vd[t]))
                    gv = jnp.where(ky[t] > float(k), gv, ZERO)
                    sum_y[t] = sum_y[t] + gv
                    obv[k, m, out_rows, TILES[t]] = vc[t] + gv
                uh = [HALF * uc[t] for t in two]
                vh = [HALF * vc[t] for t in two]
                vdh = [HALF * vd[t] for t in two]
                uwh = HALF * uw[I0]
                for scr, cen, east_col, q, run, dst in ((ts, tc, t_east, q_t, run_t, ost), (ss, sc, s_east, q_s, run_s, oss)):
                    ce = east(cen[I0], cen[I1], east_col)
                    fx = [uh[t] * (cen[t] + ce[t]) for t in two]
                    fw = west(fx[I0], fx[I1], uwh * (rot(pc, 129 - I2 * q) + cen[I0]))
                    for t in two:
                        fy = vh[t] * (cen[t] + scr[t, k, m, up, :])
                        fs = vdh[t] * (scr[t, k, m, down, :] + cen[t])
                        new = cen[t] - ((fx[t] - fw[t]) + (fy - fs))
                        new = jnp.where(kc[t] > float(k), new, ZERO)
                        run[t] = new if k == I0 else new + gain[k - I1] * run[t]
                        dst[k, m, out_rows, TILES[t]] = run[t]
            for t in two:
                sx[m, out_rows, TILES[t]] = scale_x[t] * sum_x[t]
                sy[m, out_rows, TILES[t]] = scale_y[t] * sum_y[t]
                nt = ns = zero
                for k in range(LEV - I1, -I1, -I1):
                    if k == LEV - I1:
                        coef = last[k]
                    else:
                        coef = jnp.where(kc[t] > float(k + I1), inner[k], last[k])
                    wet = kc[t] > float(k)
                    nt = jnp.where(wet, coef * ost[k, m, out_rows, TILES[t]] + gain[k] * nt, ZERO)
                    ns = jnp.where(wet, coef * oss[k, m, out_rows, TILES[t]] + gain[k] * ns, ZERO)
                    ost[k, m, out_rows, TILES[t]] = nt
                    oss[k, m, out_rows, TILES[t]] = ns
            return carry

        lax.fori_loop(I0, MEM, member, I0)

    for cp in load_copies(jnp.int32(NCH - I1)):
        cp.wait()
    lax.fori_loop(I0, MEM, prime, I0)

    def step(i, carry):
        r = ROWS // SUB - I1 - i
        c = r // BPC
        edge = lax.rem(r, BPC) == I0

        @pl.when(edge & (c >= I1))
        def _():
            for cp in load_copies(c - I1):
                cp.wait()

        @pl.when(edge & (c >= SLOTS))
        def _():
            for cp in load_copies(c - SLOTS):
                cp.start()

        @pl.when(edge & (c + I1 < NCH))
        def _():
            for cp in out_copies(c + I1):
                cp.start()

        block(r)
        return carry

    lax.fori_loop(I0, ROWS // SUB, step, I0)
    for cp in out_copies(jnp.int32(I0)):
        cp.start()
    for c in range(NCH):
        for cp in out_copies(jnp.int32(c)):
            cp.wait()


def columns_call(u, v, te, sa, px, pd, hr, dep, kmt, hx2, hrh, hrk):
    big = pltpu.VMEM((I2, LEV, MEM, EXT, LANE), F32)
    full = pltpu.VMEM((LEV, MEM, ROWS, COLS), F32)
    o3 = sds(LEV, MEM, ROWS, COLS)
    o2 = sds(MEM, ROWS, COLS)
    o1 = sds(ROWS, COLS)
    return pl.pallas_call(
        columns_kernel,
        name="columns",
        out_shape=(o3, o3, o3, o3, o2, o2, o1, o1),
        in_specs=[ANY] * 12,
        out_specs=(ANY,) * 4 + (VM,) * 4,
        scratch_shapes=[big] * 7
        + [
            pltpu.VMEM((SLOTS, 4, LEV, MEM, CHUNK, COLS), F32),
            pltpu.VMEM((MEM, NEXT, LANE), F32),
            pltpu.VMEM((I2, MEM, 4, I2, LEV, LANE), F32),
            pltpu.VMEM((I2, NEXT, LANE), F32),
            pltpu.VMEM((I2, NEXT, LANE), jnp.int32),
            pltpu.VMEM((I2, NEXT, LANE), F32),
            pltpu.VMEM((ROWS, LANE), F32),
            full, full, full, full,
            pltpu.SemaphoreType.DMA((SLOTS, 4)),
            pltpu.SemaphoreType.DMA((13,)),
            pltpu.SemaphoreType.DMA((4,)),
        ],
        compiler_params=pltpu.CompilerParams(vmem_limit_bytes=LIMIT),
    )(u, v, te, sa, px, pd, hr, dep, kmt, hx2, hrh, hrk)


def forcing_kernel(sx, sy, hxs, hds, hrx, hry, pk, send_sem, recv_sem):
    ids = neighbours()
    enter(ids)
    lane = lane_ids()
    sent = []

    def send(src, dst, who):
        i = len(sent)
        cp = pltpu.make_async_remote_copy(src_ref=src, dst_ref=dst, send_sem=send_sem.at[i], recv_sem=recv_sem.at[i], device_id=ids[who], device_id_type=MESH)
        cp.start()
        sent.append(cp)

    for r in range(ROWS // SUB):
        rows = pl.ds(SUB * r, SUB)
        for i, a in enumerate((sx, sy)):
            pk[i, rows, :] = wide_pack(lane, *[a[m, rows, t] for m in range(MEM) for t in TILES])
    for src, dst in ((sx, hrx), (sy, hry)):
        send(src.at[:, pl.ds(ROWS - HALO, HALO), :], dst.at[I0], "n")
        send(src.at[:, pl.ds(I0, HALO), :], dst.at[I1], "s")
    send(pk, hxs, "x")
    send(pk.at[:, pl.ds(ROWS - HALO, HALO), :], hds.at[I0], "nx")
    send(pk.at[:, pl.ds(I0, HALO), :], hds.at[I1], "sx")
    for cp in sent:
        cp.wait()


def forcing_call(sx, sy):
    return pl.pallas_call(
        forcing_kernel,
        name="forcing",
        out_shape=(sds(I2, ROWS, LANE), sds(I2, I2, HALO, LANE), sds(I2, MEM, HALO, COLS), sds(I2, MEM, HALO, COLS)),
        in_specs=[VM, VM],
        out_specs=(ANY,) * 4,
        scratch_shapes=[pltpu.VMEM((I2, ROWS, LANE), F32), pltpu.SemaphoreType.DMA((7,)), pltpu.SemaphoreType.DMA((7,))],
        compiler_params=pltpu.CompilerParams(collective_id=I1, has_side_effects=True, vmem_limit_bytes=LIMIT),
    )(sx, sy)


def east5(x, lane):
    last = lane == LAST
    r = [rot(a, LAST) for a in x]
    far = jnp.where(lane == 63, rot(x[I2], 63), r[4])
    return [jnp.where(last, r[I1], r[I0]), jnp.where(last, r[4], r[I1]), jnp.where(last, r[I3], r[I2]), jnp.where(last, rot(x[4], 63), r[I3]), jnp.where(last, r[I0], far)]


def west5(x, lane):
    first = lane == I0
    r = [rot(a, I1) for a in x]
    far = jnp.where(lane == 64, rot(x[I3], 65), r[4])
    return [jnp.where(first, r[4], r[I0]), jnp.where(first, r[I0], r[I1]), jnp.where(first, rot(x[4], 65), r[I2]), jnp.where(first, r[I2], r[I3]), jnp.where(first, r[I1], far)]


def east3(x, lane):
    last = lane == LAST
    r = [rot(a, LAST) for a in x]
    far = jnp.where(lane == 63, rot(x[I0], 63), r[I2])
    return [jnp.where(last, r[I1], r[I0]), jnp.where(last, r[I2], r[I1]), jnp.where(last, r[I0], far)]


SHARED = (I0, I1, I0, I1, I2)


def subcycle_kernel(weights, eta, tx, ty, sx, sy, dep, kmt, hx2, hd2, hre, hrx, hry, hrh, hrk, hxs, hds, hrsx, hrsy, eta_out, tx_out, ty_out, cx_out, cy_out, nat, side, hn, kn, e0, e1, t1, t2, f1, f2, hh, kf, gx, gy, wv, fo, acc1, acc2, tails, sem):
    row = lax.axis_index("row")
    not_south = jnp.where(row == I0, ZERO, ONE).astype(F32)
    not_north = jnp.where(row == NR - I1, ZERO, ONE).astype(F32)
    lane = lane_ids()
    base = SUB + HALO
    top = base + ROWS
    low, mid, high = pl.ds(I0, HALO), pl.ds(HALO, ROWS), pl.ds(HALO + ROWS, HALO)
    copies = []

    def fetch(src, dst):
        copies.append(pltpu.make_async_copy(src, dst, sem))

    for i, (own_, rows_) in enumerate(((eta, hre), (tx, hrx), (ty, hry), (sx, hrsx), (sy, hrsy))):
        fetch(own_, nat.at[i, :, mid, :])
        fetch(rows_.at[I0], nat.at[i, :, low, :])
        fetch(rows_.at[I1], nat.at[i, :, high, :])
    for first, count, main, corner in ((I0, 4, hx2, hd2), (4, I2, hxs, hds)):
        part = pl.ds(first, count)
        fetch(main, side.at[part, mid, :])
        fetch(corner.at[I0], side.at[part, low, :])
        fetch(corner.at[I1], side.at[part, high, :])
    for own_, rows_, dst in ((dep, hrh, hn), (kmt, hrk, kn)):
        fetch(own_, dst.at[mid, :])
        fetch(rows_.at[I0], dst.at[low, :])
        fetch(rows_.at[I1], dst.at[high, :])
    for cp in copies:
        cp.start()
    total = jnp.float32(ZERO)
    moment = jnp.float32(ZERO)
    for n in range(NSUB - I1, -I1, -I1):
        total = total + weights[n]
        moment = moment + total
        tails[n] = total
    for cp in copies:
        cp.wait()
    own = (lane < 32) | (lane >= 96)
    zero = jnp.zeros((SUB, LANE), F32)
    three, five = range(I3), range(5)
    for i in three:
        kf[i, I0:SUB, :] = zero
        kf[i, SUB + NEAR:BEXT, :] = zero
    for r in range(I1, I1 + NEAR // SUB):
        rows, here = pl.ds(SUB * r, SUB), pl.ds(SUB * r - SUB, SUB)
        packed = side[I3, here, :]
        turned = rot(packed, 64)
        levels = [kn[here, t].astype(F32) for t in TILES] + [jnp.where(own, turned, packed)]
        depths = [hn[here, t] for t in TILES] + [jnp.where(own, packed, turned)]
        keep = not_south if r < base // SUB else not_north
        inside = base // SUB <= r < top // SUB
        for i in three:
            kf[i, rows, :] = levels[i] if inside else levels[i] * keep
            hh[i, rows, :] = depths[i]

    for r in range(I1, I1 + NEAR // SUB):
        y = SUB * r
        rows, up, down, here = pl.ds(y, SUB), pl.ds(y + I1, SUB), pl.ds(y - I1, SUB), pl.ds(y - SUB, SUB)
        kc = [kf[i, rows, :] for i in three]
        ke = east3(kc, lane)
        hc = [hh[i, rows, :] for i in three]
        he = east3(hc, lane)
        wet = [kc[i] > ZERO for i in three]
        wet_x = [jnp.minimum(kc[i], ke[i]) > ZERO for i in three]
        wet_y = [jnp.minimum(kc[i], kf[i, up, :]) > ZERO for i in three]
        for i in three:
            gx[i, rows, :] = jnp.where(wet_x[i], (HALF * WAVE * WAVE) * (hc[i] + he[i]), ZERO)
            gy[i, rows, :] = jnp.where(wet_y[i], (HALF * WAVE * WAVE) * (hc[i] + hh[i, up, :]), ZERO)

        def tiles(f, mask):
            slot = f if f < I3 else f + I1
            raw = [nat[f, m, here, t] for m in range(MEM) for t in TILES] + [side[slot, here, :]]
            return [jnp.where(mask[SHARED[i]], raw[i], ZERO) for i in five]

        e = tiles(I0, wet)
        a, b = tiles(I1, wet_x), tiles(I2, wet_y)
        c, d = tiles(I3, wet_x), tiles(4, wet_y)
        aw = west5(a, lane)
        cw = west5(c, lane)
        for i in five:
            t1[i, rows, :] = a[i]
            t2[i, rows, :] = b[i]
            f1[i, rows, :] = c[i]
            f2[i, rows, :] = d[i]
            w = -WAVE * ((a[i] - aw[i]) + (b[i] - t2[i, down, :]))
            fo[i, rows, :] = -WAVE * ((c[i] - cw[i]) + (d[i] - f2[i, down, :]))
            now = e[i] + w
            wv[i, rows, :] = w
            e0[i, rows, :] = now
            acc1[i, rows, :] = weights[I0] * now
            acc2[i, rows, :] = tails[I0] * now

    def advance(src, dst, r, plan):
        y = SUB * r
        rows, up, down = pl.ds(y, SUB), pl.ds(y + I1, SUB), pl.ds(y - I1, SUB)
        now = [src[i, rows, :] for i in five]
        ne = east5(now, lane)
        gxs = [gx[i, rows, :] for i in three]
        gys = [gy[i, rows, :] for i in three]
        gyd = [gy[i, down, :] for i in three]
        fx = [gxs[SHARED[i]] * (ne[i] - now[i]) for i in five]
        fw = west5(fx, lane)
        for i in five:
            j = SHARED[i]
            w = (wv[i, rows, :] + fo[i, rows, :]) + (fx[i] - fw[i]) + (gys[j] * (src[i, up, :] - now[i]) - gyd[j] * (now[i] - src[i, down, :]))
            new = now[i] + w
            wv[i, rows, :] = w
            dst[i, rows, :] = new
            if plan is not None:
                prev, a0, b0, a1, b1 = plan
                s1, s2 = acc1[i, rows, :], acc2[i, rows, :]
                if prev:
                    s1 = s1 + a0 * now[i]
                    s2 = s2 + b0 * now[i]
                acc1[i, rows, :] = s1 + a1 * new
                acc2[i, rows, :] = s2 + b1 * new

    def sweep(src, dst, lo, hi, plan):
        for r in range(lo, hi):
            advance(src, dst, r, plan if base // SUB <= r <= top // SUB else None)

    for begin, end in ((I0, I2), (I2, 6), (6, 10), (10, 14)):
        lo = (I2 * begin + 12) // SUB
        hi = (196 - I2 * begin) // SUB + I1

        def pair(i, carry):
            m = I2 * i + I2
            sweep(e0, e1, lo, hi, None)
            sweep(e1, e0, lo, hi, (True, weights[m - I1], tails[m - I1], weights[m], tails[m]))
            return carry

        lax.fori_loop(begin, end, pair, I0)
    sweep(e0, e1, base // SUB, top // SUB + I1, (False, None, None, weights[NSUB - I1], tails[NSUB - I1]))

    for r in range(ROWS // SUB):
        y = SUB * r + base
        rows, up, out_rows = pl.ds(y, SUB), pl.ds(y + I1, SUB), pl.ds(SUB * r, SUB)
        s = [acc2[i, rows, :] for i in five]
        se = east5(s, lane)
        for m in range(MEM):
            for t in range(I2):
                i = I2 * m + t
                cols = TILES[t]
                eta_out[m, out_rows, cols] = acc1[i, rows, :]
                gxc, gyc = gx[t, rows, :], gy[t, rows, :]
                ux = total * t1[i, rows, :] + moment * f1[i, rows, :] - (ONE / WAVE) * (gxc * (se[i] - s[i]))
                uy = total * t2[i, rows, :] + moment * f2[i, rows, :] - (ONE / WAVE) * (gyc * (acc2[i, up, :] - s[i]))
                tx_out[m, out_rows, cols] = ux
                ty_out[m, out_rows, cols] = uy
                cx_out[m, out_rows, cols] = ux / jnp.where(gxc > ZERO, gxc * (ONE / (WAVE * WAVE)), ONE)
                cy_out[m, out_rows, cols] = uy / jnp.where(gyc > ZERO, gyc * (ONE / (WAVE * WAVE)), ONE)


def subcycle_call(weights, *arrays):
    o2 = sds(MEM, ROWS, COLS)
    five = pltpu.VMEM((5, BEXT, LANE), F32)
    three = pltpu.VMEM((I3, BEXT, LANE), F32)
    return pl.pallas_call(
        subcycle_kernel,
        name="subcycle",
        out_shape=(o2,) * 5,
        in_specs=[SM] + [ANY] * len(arrays),
        out_specs=(VM,) * 5,
        scratch_shapes=[
            pltpu.VMEM((5, MEM, NEAR, COLS), F32),
            pltpu.VMEM((6, NEAR, LANE), F32),
            pltpu.VMEM((NEAR, COLS), F32),
            pltpu.VMEM((NEAR, COLS), jnp.int32),
            five, five, five, five, five, five, three, three, three, three, five, five, five, five,
            pltpu.SMEM((NSUB,), F32),
            pltpu.SemaphoreType.DMA,
        ],
        compiler_params=pltpu.CompilerParams(vmem_limit_bytes=LIMIT),
    )(weights, *arrays)


DROWS = 16


def correct_kernel(bu, bv, nx, ny, cx, cy, ou, ov):
    gain, inner, last = solve_factors(VISC)

    def body(j, carry):
        m = j // (DROWS // SUB)
        rows = pl.ds(pl.multiple_of((j % (DROWS // SUB)) * SUB, SUB), SUB)
        for src, cnt, shift, dst in ((bu, nx, cx, ou), (bv, ny, cy, ov)):
            for t in range(I2):
                cols = slice(LANE * t, LANE * t + LANE)
                n = cnt[rows, cols]
                run = []
                for k in range(LEV):
                    b = src[k, m, rows, cols]
                    run.append(b if k == I0 else b + gain[k - I1] * run[-I1])
                nxt = jnp.zeros((SUB, LANE), F32)
                tot = jnp.zeros((SUB, LANE), F32)
                sol = [None] * LEV
                for k in range(LEV - I1, -I1, -I1):
                    coef = last[k] if k == LEV - I1 else jnp.where(n > float(k + I1), inner[k], last[k])
                    nxt = jnp.where(n > float(k), coef * run[k] + gain[k] * nxt, ZERO)
                    sol[k] = nxt
                    tot = tot + nxt
                add = shift[m, rows, cols] - tot / jnp.maximum(n, ONE)
                for k in range(LEV):
                    dst[k, m, rows, cols] = jnp.where(n > float(k), sol[k] + add, ZERO)
        return carry

    lax.fori_loop(I0, MEM * (DROWS // SUB), body, I0)


def correct_call(bu, bv, nx, ny, cx, cy):
    s3 = pl.BlockSpec((LEV, MEM, DROWS, COLS), lambda r: (I0, I0, r, I0))
    s2 = pl.BlockSpec((MEM, DROWS, COLS), lambda r: (I0, r, I0))
    s1 = pl.BlockSpec((DROWS, COLS), lambda r: (r, I0))
    o3 = sds(LEV, MEM, ROWS, COLS)
    return pl.pallas_call(
        correct_kernel,
        name="correct",
        grid=(ROWS // DROWS,),
        out_shape=(o3, o3),
        in_specs=[s3, s3, s1, s1, s2, s2],
        out_specs=(s3, s3),
        compiler_params=pltpu.CompilerParams(vmem_limit_bytes=LIMIT),
    )(bu, bv, nx, ny, cx, cy)


def local_step(u, v, te, sa, eta, tx, ty, dep, kmt, weights):
    px, pd, hr, hx2, hd2, hre, hrx, hry, hrh, hrk = edges_call(u, v, te, sa, eta, tx, ty, dep, kmt)
    bu, bv, ot, os, sx, sy, nx, ny = columns_call(u, v, te, sa, px, pd, hr, dep, kmt, hx2, hrh, hrk)
    hxs, hds, hrsx, hrsy = forcing_call(sx, sy)
    eta_new, tx_new, ty_new, cx, cy = subcycle_call(weights, eta, tx, ty, sx, sy, dep, kmt, hx2, hd2, hre, hrx, hry, hrh, hrk, hxs, hds, hrsx, hrsy)
    ou, ov = correct_call(bu, bv, nx, ny, cx, cy)
    return eta_new, tx_new, ty_new, ou, ov, ot, os


def solution(mesh):
    s3 = P(None, None, "row", "col")
    s2 = P(None, "row", "col")
    s1 = P("row", "col")
    return jax.shard_map(local_step, mesh=mesh, in_specs=(s3, s3, s3, s3, s2, s2, s2, s1, s1, P()), out_specs=(s2, s2, s2, s3, s3, s3, s3), check_vma=False)
```

time: 1330 us -> 149 us (0.11); the launches traced: 1320 us -> 149 us
  other arithmetic: 599 us -> 0 us
  local copies, waits for them, and re-layouts: 327 us -> 0 us
  starting transfers between devices: 210 us -> 0 us
  waiting for transfers between devices: 177 us -> 0 us
  Pallas kernels: 0 us -> 148 us
    dynamic_update_slice x128 -> x0, other arithmetic: 253 us -> none  [vertical_solve(): lax.scan(forward, (zero_level, zero_level), (lower_diag, main_diag, upper...]
    add x63 -> x0, other arithmetic: 212 us -> none  [the longest x30 86.3 us: subcycle(): ty_avg + weight * ty_now]
    ppermute x144 -> x0, starting transfers between devices: 210 us -> none  [the longest x34 83.4 us: take_south(): lax.ppermute(edge_slab, 'row', [(source, source + 1) for source in range(...]
    ppermute x144 -> x0, waiting for transfers between devices: 177 us -> none  [the longest x35 126 us: take_west(): lax.ppermute(edge_slab, 'col', [(source, (source + 1) % col_count) for so...]
    pallas_call x0 -> x5, Pallas kernels: none -> 148 us  [the longest x1 58.7 us: columns_call(): pl.pallas_call(columns_kernel, name='columns', out_shape=(o3, o3, o3, o3,...]
    slice x223 -> x0, local copies, waits for them, and re-layouts: 117 us -> none  [the longest x39 37 us: take_east(): edge_slab = field_in[..., :1]]
    mul x40 -> x0, other arithmetic: 89.3 us -> none  [the longest x30 27.9 us: subcycle(): WAVE_COURANT * depth_y * (shift_north(eta_now) - eta_now)]
    mul x64 -> x0, local copies, waits for them, and re-layouts: 63.1 us -> none  [forward(): divisor = diag_k - low_k * upper_prev]
  transfers between devices with their start and end apart: 144 -> 0, of which waited for: 60 -> 0; matrix products, arithmetic and copies ran while one was open for 53% -> 0% of each run, Pallas kernels for 0% -> 0%
where the time goes in v1:
time: 149 us
  Pallas kernels  148 us (99%)
    pallas_call x1, Pallas kernels, columns_call(): pl.pallas_call(columns_kernel, name='columns', out_shape=(o3, o3, o3, o3,...  58.7 us
    pallas_call x1, Pallas kernels, subcycle_call(): pl.pallas_call(subcycle_kernel, name='subcycle', out_shape=(o2,) * 5, in_...  48 us
    pallas_call x1, Pallas kernels, edges_call(): pl.pallas_call(edges_kernel, name='edges', out_shape=(sds(MEM, ROWS, LANE...  21.6 us
    pallas_call x1, Pallas kernels, correct_call(): pl.pallas_call(correct_kernel, name='correct', grid=(ROWS // DROWS,), out...  10.6 us
    pallas_call x1, Pallas kernels, forcing_call(): pl.pallas_call(forcing_kernel, name='forcing', out_shape=(sds(I2, ROWS, L...  9.08 us

profile of v1, /device:TPU:0, one launch (start us, length us, event | category | flops | bytes accessed | tf_op | source)
XLA Modules:
  0.0 148.7 jit_solution(8898039687303948815)
XLA Ops:
  0.6 21.6 %edges.1 = (f32[2,128,128]{2,1,0:T(8,128)}, f32[2,2,8,128]{3,2,1,0:T(8,128)}, f32[2,2,4,2,16,128]{5,4,3,2,1,0:T(8,128)}, f32[4,128,128]{2,1,0:T(8,128)}, f32[2,4...) custom-call(f32[16,2,128,256]{3,2,1,0:T(8,128)} %u.3, ...), custom_call_target="tpu_custom_call" | custom-call | tf_op jit(solution)/shard_map/edges/pallas_call | solution.py:182
  22.3 58.7 %columns.1 = (f32[16,2,128,256]{3,2,1,0:T(8,128)}, f32[16,2,128,256]{3,2,1,0:T(8,128)}, f32[16,2,128,256]{3,2,1,0:T(8,128)}, f32[16,2,128,256]{3,2,1,0:T(8,128)}...) custom-call(f32[16,2,128,256]{3,2,1,0:T(8,128)} %u.3, ...), custom_call_target="tpu_custom_call" | custom-call | tf_op jit(solution)/shard_map/columns/pallas_call | solution.py:442
  81.0 9.1 %forcing.1 = (f32[2,128,128]{2,1,0:T(8,128)}, f32[2,2,32,128]{3,2,1,0:T(8,128)}, f32[2,2,32,256]{3,2,1,0:T(8,128)}, f32[2,2,32,256]{3,2,1,0:T(8,128)}) custom-call(f32[2,128,256]{2,1,0:T(8,128)} %get-tuple-element.42.sx, f32[2,128,256]{2,1,0:T(8,128)} %get-tuple-element.43.sy), custom_call_target="tpu_custom_call" | custom-call | tf_op jit(solution)/shard_map/forcing/pallas_call | solution.py:493
  90.0 48.0 %subcycle.1 = (f32[2,128,256]{2,1,0:T(8,128)}, f32[2,128,256]{2,1,0:T(8,128)}, f32[2,128,256]{2,1,0:T(8,128)}, f32[2,128,256]{2,1,0:T(8,128)}, f32[2,128,256]{2,1,0:T(8,128)}) custom-call(f32[30]{0:T(128)} %weights.1, f32[2,128,256]{2,1,0:T(8,128)} %eta.3, f32[2,128,256]{2,1,0:T(8,128)} %tx.3, f32[2,128,256]{2,1,0:T(8,128)} %ty.3, ...), custom_call_target="tpu_custom_call" | custom-call | tf_op jit(solution)/shard_map/subcycle/pallas_call | solution.py:684
  138.1 10.6 %correct.1 = (f32[16,2,128,256]{3,2,1,0:T(8,128)}, f32[16,2,128,256]{3,2,1,0:T(8,128)}) custom-call(f32[16,2,128,256]{3,2,1,0:T(8,128)} %get-tuple-element.55.bu, f32[16,2,128,256]{3,2,1,0:T(8,128)} %get-tuple-element.56.bv, f32[128,256]{1,0:T(8,128)} %get-tuple-element.57.nx, f32[128,256]{1,0:T(8,128)} %get-tuple-element.58.ny, ...), custom_call_target="tpu_custom_call" | custom-call | tf_op jit(solution)/shard_map/correct/pallas_call | solution.py:741

commit v2 on v1

--- a/solution.py
+++ b/solution.py
@@ -36,6 +36,7 @@
 NCH = ROWS // CHUNK
 SLOTS = I3
 BPC = CHUNK // SUB
+DEPTH = I3
 MESH = pl.DeviceIdType.MESH
 LIMIT = 67043328
 TILES = (slice(I0, LANE), slice(LANE, 256))
@@ -207,7 +208,7 @@
     )(u, v, te, sa, eta, tx, ty, dep, kmt)
 
 
-def columns_kernel(u, v, te, sa, px, pd, hr, dep, kmt, hx2, hrh, hrk, bu, bv, ot, os, sx, sy, nx, ny, us, vs, ts, ss, ps, vel, uwl, stage, pxs, hrs, hs, ki, kf, hks, obu, obv, ost, oss, load_sem, misc_sem, out_sem):
+def columns_kernel(u, v, te, sa, px, pd, hr, dep, kmt, hx2, hrh, hrk, bu, bv, ot, os, sx, sy, nx, ny, us, vs, ts, ss, ps, vel, uwl, sides, stage, pxs, hrs, hs, ki, kf, hks, obu, obv, ost, oss, load_sem, misc_sem, out_sem):
     row = lax.axis_index("row")
     not_south = jnp.where(row == I0, ZERO, ONE).astype(F32)
     not_north = jnp.where(row == NR - I1, ZERO, ONE).astype(F32)
@@ -267,32 +268,53 @@
         ra, rb = rot(a, LAST), rot(b, LAST)
         return jnp.where(is_last, rb, ra), jnp.where(is_last, halo, rb)
 
-    def west(a, b, halo):
-        ra, rb = rot(a, I1), rot(b, I1)
-        return jnp.where(is_first, halo, ra), jnp.where(is_first, ra, rb)
-
-    def keep_east(m, k, rows, a, b, edge):
-        for t, x in enumerate(east(a, b, rot(edge, LAST - I2 * (LEV + k)))):
-            vel[t, k, m, rows, :] = x
+    def push(x, edge, q):
+        return [rot(a, LAST) for a in x] + [rot(edge, LAST - I2 * q)], [rot(a, I1) for a in x] + [rot(edge, 129 - I2 * q)]
+
+    def pop_east(east_):
+        return jnp.where(is_last, east_[I1], east_[I0]), jnp.where(is_last, east_[I2], east_[I1])
+
+    def pop_west(west_):
+        return jnp.where(is_first, west_[I2], west_[I0]), jnp.where(is_first, west_[I0], west_[I1])
 
     def unpack(r, m, k, edge):
         slot = lax.rem(jnp.maximum(r, I0) // BPC, SLOTS)
         src_rows = pl.ds(pl.multiple_of(SUB * lax.rem(jnp.maximum(r, I0), BPC), SUB), SUB)
         dst_rows = pl.ds(pl.multiple_of(jnp.where(r < I0, NEXT, SUB * r + SUB), SUB), SUB)
+        rolled = []
         for f, (_, dst) in enumerate(fields):
             x = [stage[slot, f, k, m, src_rows, TILES[t]] for t in two]
             for t in two:
                 dst[t, k, m, dst_rows, :] = x[t]
-            if f == I1:
-                keep_east(m, k, dst_rows, x[I0], x[I1], edge)
+            rolled.append(push(x, edge, f * LEV + k))
+        return rolled
+
+    def settle(r, m, k, rolled):
+        dst_rows = pl.ds(pl.multiple_of(jnp.where(r < I0, NEXT, SUB * r + SUB), SUB), SUB)
+        ring = lax.rem(r + I2, I2)
+        for f in range(4):
+            east_, west_ = pop_east(rolled[f][I0]), pop_west(rolled[f][I1])
+            for t in two:
+                if f == I0:
+                    sides[I0, ring, t, k, m, :, :] = east_[t]
+                    uwl[t, k, m, dst_rows, :] = west_[t]
+                elif f == I1:
+                    vel[t, k, m, dst_rows, :] = east_[t]
+                    sides[I1, ring, t, k, m, :, :] = west_[t]
+                else:
+                    sides[I2 * f - I2, ring, t, k, m, :, :] = east_[t]
+                    sides[I2 * f - I1, ring, t, k, m, :, :] = west_[t]
 
     def prime(m, carry):
         south, north, first = pl.ds(I0, SUB), pl.ds(SUB + ROWS, SUB), pl.ds(ROWS, SUB)
         below = [zero, zero]
         for k in range(LEV):
-            unpack(jnp.int32(ROWS // SUB - I1), m, k, pxs[m, first, :])
-            keep_east(m, k, south, vs[I0, k, m, south, :], vs[I1, k, m, south, :], pxs[m, south, :])
-            for t, x in enumerate(west(us[I0, k, m, north, :], us[I1, k, m, north, :], rot(pxs[m, north, :], 129 - I2 * k))):
+            settle(jnp.int32(ROWS // SUB - I1), m, k, unpack(jnp.int32(ROWS // SUB - I1), m, k, pxs[m, first, :]))
+            v_side = push([vs[t, k, m, south, :] for t in two], pxs[m, south, :], LEV + k)[I0]
+            u_side = push([us[t, k, m, north, :] for t in two], pxs[m, north, :], k)[I1]
+            for t, x in enumerate(pop_east(v_side)):
+                vel[t, k, m, south, :] = x
+            for t, x in enumerate(pop_west(u_side)):
                 uwl[t, k, m, north, :] = x
             for t in two:
                 half = (HALF * rho_s) * ss[t, k, m, north, :] - (HALF * rho_t) * ts[t, k, m, north, :]
@@ -321,63 +343,52 @@
             scale_x.append(jnp.where(kx[t] > ZERO, HALF * (hc[t] + he[t]), ZERO) / (jnp.maximum(kx[t], ONE) * NSUB))
             scale_y.append(jnp.where(ky[t] > ZERO, HALF * (hc[t] + hs[t, up, :]), ZERO) / (jnp.maximum(ky[t], ONE) * NSUB))
 
+        ring = lax.rem(r, I2)
+
         def member(m, carry):
-            pc = pxs[m, rows, :]
             edge = pxs[m, south, :]
-            below = [zero, zero, zero]
+            below = [zero] * 4
             sum_x = [zero, zero]
             sum_y = [zero, zero]
             run_t = [None, None]
             run_s = [None, None]
-            for k in range(LEV):
-                unpack(r - I1, m, k, edge)
-                q_u, q_v, q_t, q_s = k, LEV + k, I2 * LEV + k, I3 * LEV + k
-                uc = [us[t, k, m, rows, :] for t in two]
-                vc = [vs[t, k, m, rows, :] for t in two]
-                vd = [vs[t, k, m, down, :] for t in two]
-                tc = [ts[t, k, m, rows, :] for t in two]
-                sc = [ss[t, k, m, rows, :] for t in two]
-                t_east = rot(pc, LAST - I2 * q_t)
-                s_east = rot(pc, LAST - I2 * q_s)
-                press = []
-                for i, (a, b) in enumerate(((tc[I0], sc[I0]), (tc[I1], sc[I1]), (t_east, s_east))):
-                    half = (HALF * rho_s) * b - (HALF * rho_t) * a
-                    now = below[i] + half
-                    below[i] = now + half
-                    press.append(now)
-                pe = east(press[I0], press[I1], press[I2])
-                ue = east(uc[I0], uc[I1], rot(pc, LAST - I2 * q_u))
-                uw = west(uc[I0], uc[I1], rot(pc, 129 - I2 * q_u))
-                vw = west(vc[I0], vc[I1], rot(pc, 129 - I2 * q_v))
-                ve = [vel[t, k, m, rows, :] for t in two]
+            waiting = []
+            for ahead in range(LEV + DEPTH):
+                if ahead < LEV:
+                    waiting.append(unpack(r - I1, m, ahead, edge))
+                k = ahead - DEPTH
+                if k < I0:
+                    continue
+                settle(r - I1, m, k, waiting.pop(I0))
                 for t in two:
-                    ps[t, k, m, rows, :] = press[t]
-                    uwl[t, k, m, rows, :] = uw[t]
-                for t in two:
-                    un, ud = us[t, k, m, up, :], us[t, k, m, down, :]
-                    vq = (vc[t] + vd[t]) + (ve[t] + vel[t, k, m, down, :])
-                    uq = (uc[t] + un) + (uw[t] + uwl[t, k, m, up, :])
-                    gu = (press[t] - pe[t]) - HALF * (uc[t] * (ue[t] - uw[t])) - 0.125 * (vq * (un - ud))
+                    uc, un, ud = us[t, k, m, rows, :], us[t, k, m, up, :], us[t, k, m, down, :]
+                    vc, vn, vd = vs[t, k, m, rows, :], vs[t, k, m, up, :], vs[t, k, m, down, :]
+                    tc, sc = ts[t, k, m, rows, :], ss[t, k, m, rows, :]
+                    ue, vw, t_e, t_w, s_e, s_w = [sides[i, ring, t, k, m, :, :] for i in range(6)]
+                    uw, ve = uwl[t, k, m, rows, :], vel[t, k, m, rows, :]
+                    half = (HALF * rho_s) * sc - (HALF * rho_t) * tc
+                    press = below[t] + half
+                    below[t] = press + half
+                    half = (HALF * rho_s) * s_e - (HALF * rho_t) * t_e
+                    press_e = below[I2 + t] + half
+                    below[I2 + t] = press_e + half
+                    ps[t, k, m, rows, :] = press
+                    uh, vh, vdh, uwh = HALF * uc, HALF * vc, HALF * vd, HALF * uw
+                    vq = (vc + vd) + (ve + vel[t, k, m, down, :])
+                    uq = (uc + un) + (uw + uwl[t, k, m, up, :])
+                    gu = (press - press_e) - uh * (ue - uw) - 0.125 * (vq * (un - ud))
                     gu = jnp.where(kx[t] > float(k), gu, ZERO)
                     sum_x[t] = sum_x[t] + gu
-                    obu[k, m, out_rows, TILES[t]] = uc[t] + gu
-                    gv = (press[t] - ps[t, k, m, up, :]) - 0.125 * (uq * (ve[t] - vw[t])) - HALF * (vc[t] * (vs[t, k, m, up, :] - vd[t]))
+                    obu[k, m, out_rows, TILES[t]] = uc + gu
+                    gv = (press - ps[t, k, m, up, :]) - 0.125 * (uq * (ve - vw)) - vh * (vn - vd)
                     gv = jnp.where(ky[t] > float(k), gv, ZERO)
                     sum_y[t] = sum_y[t] + gv
-                    obv[k, m, out_rows, TILES[t]] = vc[t] + gv
-                uh = [HALF * uc[t] for t in two]
-                vh = [HALF * vc[t] for t in two]
-                vdh = [HALF * vd[t] for t in two]
-                uwh = HALF * uw[I0]
-                for scr, cen, east_col, q, run, dst in ((ts, tc, t_east, q_t, run_t, ost), (ss, sc, s_east, q_s, run_s, oss)):
-                    ce = east(cen[I0], cen[I1], east_col)
-                    fx = [uh[t] * (cen[t] + ce[t]) for t in two]
-                    fw = west(fx[I0], fx[I1], uwh * (rot(pc, 129 - I2 * q) + cen[I0]))
-                    for t in two:
-                        fy = vh[t] * (cen[t] + scr[t, k, m, up, :])
-                        fs = vdh[t] * (scr[t, k, m, down, :] + cen[t])
-                        new = cen[t] - ((fx[t] - fw[t]) + (fy - fs))
-                        new = jnp.where(kc[t] > float(k), new, ZERO)
+                    obv[k, m, out_rows, TILES[t]] = vc + gv
+                    wet = kc[t] > float(k)
+                    for scr, cen, e, w, run, dst in ((ts, tc, t_e, t_w, run_t, ost), (ss, sc, s_e, s_w, run_s, oss)):
+                        fx = uh * (cen + e) - uwh * (w + cen)
+                        fy = vh * (cen + scr[t, k, m, up, :]) - vdh * (scr[t, k, m, down, :] + cen)
+                        new = jnp.where(wet, cen - (fx + fy), ZERO)
                         run[t] = new if k == I0 else new + gain[k - I1] * run[t]
                         dst[k, m, out_rows, TILES[t]] = run[t]
             for t in two:
@@ -447,6 +458,7 @@
         out_specs=(ANY,) * 4 + (VM,) * 4,
         scratch_shapes=[big] * 7
         + [
+            pltpu.VMEM((6, I2, I2, LEV, MEM, SUB, LANE), F32),
             pltpu.VMEM((SLOTS, 4, LEV, MEM, CHUNK, COLS), F32),
             pltpu.VMEM((MEM, NEXT, LANE), F32),
             pltpu.VMEM((I2, MEM, 4, I2, LEV, LANE), F32),
@@ -501,31 +513,60 @@
     )(sx, sy)
 
 
-def east5(x, lane):
+def turn_east(x):
+    return [rot(a, LAST) for a in x] + [rot(x[I2], 63), rot(x[4], 63)]
+
+
+def pick_east(r, lane):
     last = lane == LAST
-    r = [rot(a, LAST) for a in x]
-    far = jnp.where(lane == 63, rot(x[I2], 63), r[4])
-    return [jnp.where(last, r[I1], r[I0]), jnp.where(last, r[4], r[I1]), jnp.where(last, r[I3], r[I2]), jnp.where(last, rot(x[4], 63), r[I3]), jnp.where(last, r[I0], far)]
-
-
-def west5(x, lane):
+    far = jnp.where(lane == 63, r[5], r[4])
+    return [jnp.where(last, r[I1], r[I0]), jnp.where(last, r[4], r[I1]), jnp.where(last, r[I3], r[I2]), jnp.where(last, r[6], r[I3]), jnp.where(last, r[I0], far)]
+
+
+def turn_west(x):
+    return [rot(a, I1) for a in x] + [rot(x[I3], 65), rot(x[4], 65)]
+
+
+def pick_west(r, lane):
     first = lane == I0
-    r = [rot(a, I1) for a in x]
-    far = jnp.where(lane == 64, rot(x[I3], 65), r[4])
-    return [jnp.where(first, r[4], r[I0]), jnp.where(first, r[I0], r[I1]), jnp.where(first, rot(x[4], 65), r[I2]), jnp.where(first, r[I2], r[I3]), jnp.where(first, r[I1], far)]
-
-
-def east3(x, lane):
+    far = jnp.where(lane == 64, r[5], r[4])
+    return [jnp.where(first, r[4], r[I0]), jnp.where(first, r[I0], r[I1]), jnp.where(first, r[6], r[I2]), jnp.where(first, r[I2], r[I3]), jnp.where(first, r[I1], far)]
+
+
+def turn_east3(x):
+    return [rot(a, LAST) for a in x] + [rot(x[I0], 63)]
+
+
+def pick_east3(r, lane):
     last = lane == LAST
-    r = [rot(a, LAST) for a in x]
-    far = jnp.where(lane == 63, rot(x[I0], 63), r[I2])
+    far = jnp.where(lane == 63, r[I3], r[I2])
     return [jnp.where(last, r[I1], r[I0]), jnp.where(last, r[I2], r[I1]), jnp.where(last, r[I0], far)]
 
 
+def turn_west3(x):
+    return [rot(a, I1) for a in x] + [rot(x[I1], 65)]
+
+
+def pick_west3(r, lane):
+    first = lane == I0
+    far = jnp.where(lane == 64, r[I3], r[I2])
+    return [jnp.where(first, r[I2], r[I0]), jnp.where(first, r[I0], r[I1]), jnp.where(first, r[I1], far)]
+
+
+def staged(items, issue, finish, depth):
+    queue = []
+    for item in items:
+        queue.append((item, issue(item)))
+        if len(queue) > depth:
+            finish(*queue.pop(I0))
+    for item, value in queue:
+        finish(item, value)
+
+
 SHARED = (I0, I1, I0, I1, I2)
 
 
-def subcycle_kernel(weights, eta, tx, ty, sx, sy, dep, kmt, hx2, hd2, hre, hrx, hry, hrh, hrk, hxs, hds, hrsx, hrsy, eta_out, tx_out, ty_out, cx_out, cy_out, nat, side, hn, kn, e0, e1, t1, t2, f1, f2, hh, kf, gx, gy, wv, fo, acc1, acc2, tails, sem):
+def subcycle_kernel(weights, eta, tx, ty, sx, sy, dep, kmt, hx2, hd2, hre, hrx, hry, hrh, hrk, hxs, hds, hrsx, hrsy, eta_out, tx_out, ty_out, cx_out, cy_out, nat, side, hn, kn, e0, e1, t1, t2, f1, f2, hh, kf, gx, gy, gxw, gc, wv, fo, acc1, acc2, ee, ew, tails, sem):
     row = lax.axis_index("row")
     not_south = jnp.where(row == I0, ZERO, ONE).astype(F32)
     not_north = jnp.where(row == NR - I1, ZERO, ONE).astype(F32)
@@ -567,10 +608,19 @@
     for i in three:
         kf[i, I0:SUB, :] = zero
         kf[i, SUB + NEAR:BEXT, :] = zero
-    for r in range(I1, I1 + NEAR // SUB):
-        rows, here = pl.ds(SUB * r, SUB), pl.ds(SUB * r - SUB, SUB)
+    everything = range(I1, I1 + NEAR // SUB)
+
+    def rows_of(r):
+        return pl.ds(SUB * r, SUB), pl.ds(SUB * r + I1, SUB), pl.ds(SUB * r - I1, SUB), pl.ds(SUB * r - SUB, SUB)
+
+    def level_issue(r):
+        here = rows_of(r)[I3]
         packed = side[I3, here, :]
-        turned = rot(packed, 64)
+        return packed, rot(packed, 64)
+
+    def level_finish(r, value):
+        packed, turned = value
+        rows, _, _, here = rows_of(r)
         levels = [kn[here, t].astype(F32) for t in TILES] + [jnp.where(own, turned, packed)]
         depths = [hn[here, t] for t in TILES] + [jnp.where(own, packed, turned)]
         keep = not_south if r < base // SUB else not_north
@@ -579,71 +629,103 @@
             kf[i, rows, :] = levels[i] if inside else levels[i] * keep
             hh[i, rows, :] = depths[i]
 
-    for r in range(I1, I1 + NEAR // SUB):
-        y = SUB * r
-        rows, up, down, here = pl.ds(y, SUB), pl.ds(y + I1, SUB), pl.ds(y - I1, SUB), pl.ds(y - SUB, SUB)
+    staged(everything, level_issue, level_finish, SUB)
+
+    def mask_issue(r):
+        rows = rows_of(r)[I0]
         kc = [kf[i, rows, :] for i in three]
-        ke = east3(kc, lane)
         hc = [hh[i, rows, :] for i in three]
-        he = east3(hc, lane)
+        return kc, hc, turn_east3(kc), turn_east3(hc)
+
+    def mask_finish(r, value):
+        kc, hc, kt, ht = value
+        rows, up, down, here = rows_of(r)
+        ke, he = pick_east3(kt, lane), pick_east3(ht, lane)
         wet = [kc[i] > ZERO for i in three]
         wet_x = [jnp.minimum(kc[i], ke[i]) > ZERO for i in three]
         wet_y = [jnp.minimum(kc[i], kf[i, up, :]) > ZERO for i in three]
         for i in three:
             gx[i, rows, :] = jnp.where(wet_x[i], (HALF * WAVE * WAVE) * (hc[i] + he[i]), ZERO)
             gy[i, rows, :] = jnp.where(wet_y[i], (HALF * WAVE * WAVE) * (hc[i] + hh[i, up, :]), ZERO)
-
-        def tiles(f, mask):
+        for f, mask, dst in ((I0, wet, e0), (I1, wet_x, t1), (I2, wet_y, t2), (I3, wet_x, f1), (4, wet_y, f2)):
             slot = f if f < I3 else f + I1
             raw = [nat[f, m, here, t] for m in range(MEM) for t in TILES] + [side[slot, here, :]]
-            return [jnp.where(mask[SHARED[i]], raw[i], ZERO) for i in five]
-
-        e = tiles(I0, wet)
-        a, b = tiles(I1, wet_x), tiles(I2, wet_y)
-        c, d = tiles(I3, wet_x), tiles(4, wet_y)
-        aw = west5(a, lane)
-        cw = west5(c, lane)
+            for i in five:
+                dst[i, rows, :] = jnp.where(mask[SHARED[i]], raw[i], ZERO)
+
+    staged(everything, mask_issue, mask_finish, I3)
+
+    def start_issue(r):
+        rows = rows_of(r)[I0]
+        a = [t1[i, rows, :] for i in five]
+        c = [f1[i, rows, :] for i in five]
+        return a, c, turn_west(a), turn_west(c), turn_west3([gx[i, rows, :] for i in three])
+
+    late = []
+
+    def start_finish(r, value):
+        a, c, at, ct, gt = value
+        rows, up, down, here = rows_of(r)
+        aw, cw, gw = pick_west(at, lane), pick_west(ct, lane), pick_west3(gt, lane)
+        for i in three:
+            gxw[i, rows, :] = gw[i]
+            gc[i, rows, :] = (gx[i, rows, :] + gw[i]) + (gy[i, rows, :] + gy[i, down, :])
+        fresh = []
         for i in five:
-            t1[i, rows, :] = a[i]
-            t2[i, rows, :] = b[i]
-            f1[i, rows, :] = c[i]
-            f2[i, rows, :] = d[i]
-            w = -WAVE * ((a[i] - aw[i]) + (b[i] - t2[i, down, :]))
-            fo[i, rows, :] = -WAVE * ((c[i] - cw[i]) + (d[i] - f2[i, down, :]))
-            now = e[i] + w
+            w = -WAVE * ((a[i] - aw[i]) + (t2[i, rows, :] - t2[i, down, :]))
+            fo[i, rows, :] = -WAVE * ((c[i] - cw[i]) + (f2[i, rows, :] - f2[i, down, :]))
+            now = e0[i, rows, :] + w
             wv[i, rows, :] = w
             e0[i, rows, :] = now
             acc1[i, rows, :] = weights[I0] * now
             acc2[i, rows, :] = tails[I0] * now
-
-    def advance(src, dst, r, plan):
-        y = SUB * r
-        rows, up, down = pl.ds(y, SUB), pl.ds(y + I1, SUB), pl.ds(y - I1, SUB)
-        now = [src[i, rows, :] for i in five]
-        ne = east5(now, lane)
-        gxs = [gx[i, rows, :] for i in three]
-        gys = [gy[i, rows, :] for i in three]
-        gyd = [gy[i, down, :] for i in three]
-        fx = [gxs[SHARED[i]] * (ne[i] - now[i]) for i in five]
-        fw = west5(fx, lane)
+            fresh.append(now)
+        late.append((r, turn_east(fresh), turn_west(fresh)))
+        if len(late) > I3:
+            store_sides(*late.pop(I0), I0)
+
+    def store_sides(r, et, wt, buf):
+        rows = rows_of(r)[I0]
+        ne, nw = pick_east(et, lane), pick_west(wt, lane)
+        for i in five:
+            ee[buf, i, rows, :] = ne[i]
+            ew[buf, i, rows, :] = nw[i]
+
+    staged(everything, start_issue, start_finish, I3)
+    for item in late:
+        store_sides(*item, I0)
+
+    def advance(src, buf, dst, r, plan):
+        rows, up, down, _ = rows_of(r)
+        gxc, gxm, gyc, gyd, gcc = [[g[i, rows_, :] for i in three] for g, rows_ in ((gx, rows), (gxw, rows), (gy, rows), (gy, down), (gc, rows))]
+        fresh = []
         for i in five:
             j = SHARED[i]
-            w = (wv[i, rows, :] + fo[i, rows, :]) + (fx[i] - fw[i]) + (gys[j] * (src[i, up, :] - now[i]) - gyd[j] * (now[i] - src[i, down, :]))
-            new = now[i] + w
+            now = src[i, rows, :]
+            w = (wv[i, rows, :] + fo[i, rows, :]) - gcc[j] * now
+            w = w + ((gxc[j] * ee[buf, i, rows, :] + gxm[j] * ew[buf, i, rows, :]) + (gyc[j] * src[i, up, :] + gyd[j] * src[i, down, :]))
+            new = now + w
             wv[i, rows, :] = w
             dst[i, rows, :] = new
+            fresh.append(new)
             if plan is not None:
                 prev, a0, b0, a1, b1 = plan
                 s1, s2 = acc1[i, rows, :], acc2[i, rows, :]
                 if prev:
-                    s1 = s1 + a0 * now[i]
-                    s2 = s2 + b0 * now[i]
+                    s1 = s1 + a0 * now
+                    s2 = s2 + b0 * now
                 acc1[i, rows, :] = s1 + a1 * new
                 acc2[i, rows, :] = s2 + b1 * new
-
-    def sweep(src, dst, lo, hi, plan):
-        for r in range(lo, hi):
-            advance(src, dst, r, plan if base // SUB <= r <= top // SUB else None)
+        return turn_east(fresh), turn_west(fresh)
+
+    def sweep(src, buf, dst, lo, hi, plan, depth=I3):
+        def issue(r):
+            return advance(src, buf, dst, r, plan if base // SUB <= r <= top // SUB else None)
+
+        def finish(r, value):
+            store_sides(r, *value, I1 - buf)
+
+        staged(range(lo, hi), issue, finish, depth)
 
     for begin, end in ((I0, I2), (I2, 6), (6, 10), (10, 14)):
         lo = (I2 * begin + 12) // SUB
@@ -651,18 +733,23 @@
 
         def pair(i, carry):
             m = I2 * i + I2
-            sweep(e0, e1, lo, hi, None)
-            sweep(e1, e0, lo, hi, (True, weights[m - I1], tails[m - I1], weights[m], tails[m]))
+            sweep(e0, I0, e1, lo, hi, None)
+            sweep(e1, I1, e0, lo, hi, (True, weights[m - I1], tails[m - I1], weights[m], tails[m]))
             return carry
 
         lax.fori_loop(begin, end, pair, I0)
-    sweep(e0, e1, base // SUB, top // SUB + I1, (False, None, None, weights[NSUB - I1], tails[NSUB - I1]))
-
-    for r in range(ROWS // SUB):
-        y = SUB * r + base
-        rows, up, out_rows = pl.ds(y, SUB), pl.ds(y + I1, SUB), pl.ds(SUB * r, SUB)
+    sweep(e0, I0, e1, base // SUB, top // SUB + I1, (False, None, None, weights[NSUB - I1], tails[NSUB - I1]))
+
+    def end_issue(r):
+        rows = rows_of(r)[I0]
         s = [acc2[i, rows, :] for i in five]
-        se = east5(s, lane)
+        return s, turn_east(s)
+
+    def end_finish(r, value):
+        s, st = value
+        rows, up, _, _ = rows_of(r)
+        out_rows = pl.ds(SUB * r - base, SUB)
+        se = pick_east(st, lane)
         for m in range(MEM):
             for t in range(I2):
                 i = I2 * m + t
@@ -675,6 +762,8 @@
                 ty_out[m, out_rows, cols] = uy
                 cx_out[m, out_rows, cols] = ux / jnp.where(gxc > ZERO, gxc * (ONE / (WAVE * WAVE)), ONE)
                 cy_out[m, out_rows, cols] = uy / jnp.where(gyc > ZERO, gyc * (ONE / (WAVE * WAVE)), ONE)
+
+    staged(range(base // SUB, top // SUB), end_issue, end_finish, I3)
 
 
 def subcycle_call(weights, *arrays):
@@ -692,7 +781,7 @@
             pltpu.VMEM((6, NEAR, LANE), F32),
             pltpu.VMEM((NEAR, COLS), F32),
             pltpu.VMEM((NEAR, COLS), jnp.int32),
-            five, five, five, five, five, five, three, three, three, three, five, five, five, five,
+            *[five] * 6, *[three] * 6, *[five] * 4, pltpu.VMEM((I2, 5, BEXT, LANE), F32), pltpu.VMEM((I2, 5, BEXT, LANE), F32),
             pltpu.SMEM((NSUB,), F32),
             pltpu.SemaphoreType.DMA,
         ],

time: 149 us -> 91.7 us (0.62)
  Pallas kernels: 148 us -> 90.7 us
    pallas_call x1, Pallas kernels: 48 us -> 16.4 us  [subcycle_call(): pl.pallas_call(subcycle_kernel, name='subcycle', out_shape=(o2,) * 5, in_...]
    pallas_call x1, Pallas kernels: 58.7 us -> 33 us  [columns_call(): pl.pallas_call(columns_kernel, name='columns', out_shape=(o3, o3, o3, o3,...]
where the time goes in v2:
time: 91.7 us; the launch traced here: 91.4 us
  Pallas kernels  90.7 us (99%)
    pallas_call x1, Pallas kernels, columns_call(): pl.pallas_call(columns_kernel, name='columns', out_shape=(o3, o3, o3, o3,...  33 us
    pallas_call x1, Pallas kernels, edges_call(): pl.pallas_call(edges_kernel, name='edges', out_shape=(sds(MEM, ROWS, LANE...  21.6 us
    pallas_call x1, Pallas kernels, subcycle_call(): pl.pallas_call(subcycle_kernel, name='subcycle', out_shape=(o2,) * 5, in_...  16.4 us
    pallas_call x1, Pallas kernels, correct_call(): pl.pallas_call(correct_kernel, name='correct', grid=(ROWS // DROWS,), out...  10.6 us
    pallas_call x1, Pallas kernels, forcing_call(): pl.pallas_call(forcing_kernel, name='forcing', out_shape=(sds(I2, ROWS, L...  9.08 us

profile of v2, /device:TPU:0, one launch (start us, length us, event | category | flops | bytes accessed | tf_op | source)
XLA Modules:
  0.0 91.4 jit_solution(3216705846775218942)
XLA Ops:
  0.6 21.6 %edges.1 = (f32[2,128,128]{2,1,0:T(8,128)}, f32[2,2,8,128]{3,2,1,0:T(8,128)}, f32[2,2,4,2,16,128]{5,4,3,2,1,0:T(8,128)}, f32[4,128,128]{2,1,0:T(8,128)}, f32[2,4...) custom-call(f32[16,2,128,256]{3,2,1,0:T(8,128)} %u.3, ...), custom_call_target="tpu_custom_call" | custom-call | tf_op jit(solution)/shard_map/edges/pallas_call | solution.py:183
  22.3 33.0 %columns.1 = (f32[16,2,128,256]{3,2,1,0:T(8,128)}, f32[16,2,128,256]{3,2,1,0:T(8,128)}, f32[16,2,128,256]{3,2,1,0:T(8,128)}, f32[16,2,128,256]{3,2,1,0:T(8,128)}...) custom-call(f32[16,2,128,256]{3,2,1,0:T(8,128)} %u.3, ...), custom_call_target="tpu_custom_call" | custom-call | tf_op jit(solution)/shard_map/columns/pallas_call | solution.py:453
  55.2 9.1 %forcing.1 = (f32[2,128,128]{2,1,0:T(8,128)}, f32[2,2,32,128]{3,2,1,0:T(8,128)}, f32[2,2,32,256]{3,2,1,0:T(8,128)}, f32[2,2,32,256]{3,2,1,0:T(8,128)}) custom-call(f32[2,128,256]{2,1,0:T(8,128)} %get-tuple-element.42.sx, f32[2,128,256]{2,1,0:T(8,128)} %get-tuple-element.43.sy), custom_call_target="tpu_custom_call" | custom-call | tf_op jit(solution)/shard_map/forcing/pallas_call | solution.py:505
  64.3 16.4 %subcycle.1 = (f32[2,128,256]{2,1,0:T(8,128)}, f32[2,128,256]{2,1,0:T(8,128)}, f32[2,128,256]{2,1,0:T(8,128)}, f32[2,128,256]{2,1,0:T(8,128)}, f32[2,128,256]{2,1,0:T(8,128)}) custom-call(f32[30]{0:T(128)} %weights.1, f32[2,128,256]{2,1,0:T(8,128)} %eta.3, f32[2,128,256]{2,1,0:T(8,128)} %tx.3, f32[2,128,256]{2,1,0:T(8,128)} %ty.3, ...), custom_call_target="tpu_custom_call" | custom-call | tf_op jit(solution)/shard_map/subcycle/pallas_call | solution.py:773
  80.8 10.6 %correct.1 = (f32[16,2,128,256]{3,2,1,0:T(8,128)}, f32[16,2,128,256]{3,2,1,0:T(8,128)}) custom-call(f32[16,2,128,256]{3,2,1,0:T(8,128)} %get-tuple-element.55.bu, f32[16,2,128,256]{3,2,1,0:T(8,128)} %get-tuple-element.56.bv, f32[128,256]{1,0:T(8,128)} %get-tuple-element.57.nx, f32[128,256]{1,0:T(8,128)} %get-tuple-element.58.ny, ...), custom_call_target="tpu_custom_call" | custom-call | tf_op jit(solution)/shard_map/correct/pallas_call | solution.py:830

commit v3 on v2

--- a/solution.py
+++ b/solution.py
@@ -36,7 +36,7 @@
 NCH = ROWS // CHUNK
 SLOTS = I3
 BPC = CHUNK // SUB
-DEPTH = I3
+DEPTH = I2
 MESH = pl.DeviceIdType.MESH
 LIMIT = 67043328
 TILES = (slice(I0, LANE), slice(LANE, 256))
@@ -58,6 +58,11 @@
         prev = strength / diag
         gain.append(prev)
     return gain, inner, last
+
+
+def level_factor(count, k, inner, last):
+    edge = jnp.where(count > float(k), last[k], ZERO)
+    return edge if k == LEV - I1 else jnp.where(count > float(k + I1), inner[k], edge)
 
 
 def lane_ids():
@@ -112,6 +117,7 @@
         cp = pltpu.make_async_remote_copy(src_ref=src, dst_ref=dst, send_sem=send_sem.at[i], recv_sem=recv_sem.at[i], device_id=ids[who], device_id_type=MESH)
         cp.start()
         sent.append(cp)
+        return cp
 
     for src, dst in ((eta, hre), (tx, hrx), (ty, hry)):
         send(src.at[:, pl.ds(ROWS - HALO, HALO), :], dst.at[I0], "n")
@@ -161,15 +167,17 @@
         send(rowb.at[I0, m], hr.at[I0, m], "n")
         send(rowb.at[I1, m], hr.at[I1, m], "s")
 
-    send(pk2, hx2, "x")
-    send(pk2.at[:, pl.ds(ROWS - HALO, HALO), :], hd2.at[I0], "nx")
-    send(pk2.at[:, pl.ds(I0, HALO), :], hd2.at[I1], "sx")
+    side = send(pk2, hx2, "x")
     pack3(I0)
     send3(I0)
     pack3(I1)
     send3(I1)
+    side.wait()
+    send(hx2.at[:, pl.ds(ROWS - HALO, HALO), :], hd2.at[I0], "n")
+    send(hx2.at[:, pl.ds(I0, HALO), :], hd2.at[I1], "s")
     for cp in sent:
-        cp.wait()
+        if cp is not side:
+            cp.wait()
 
 
 def sds(*shape, dtype=F32):
@@ -396,13 +404,9 @@
                 sy[m, out_rows, TILES[t]] = scale_y[t] * sum_y[t]
                 nt = ns = zero
                 for k in range(LEV - I1, -I1, -I1):
-                    if k == LEV - I1:
-                        coef = last[k]
-                    else:
-                        coef = jnp.where(kc[t] > float(k + I1), inner[k], last[k])
-                    wet = kc[t] > float(k)
-                    nt = jnp.where(wet, coef * ost[k, m, out_rows, TILES[t]] + gain[k] * nt, ZERO)
-                    ns = jnp.where(wet, coef * oss[k, m, out_rows, TILES[t]] + gain[k] * ns, ZERO)
+                    coef = level_factor(kc[t], k, inner, last)
+                    nt = coef * ost[k, m, out_rows, TILES[t]] + gain[k] * nt
+                    ns = coef * oss[k, m, out_rows, TILES[t]] + gain[k] * ns
                     ost[k, m, out_rows, TILES[t]] = nt
                     oss[k, m, out_rows, TILES[t]] = ns
             return carry
@@ -796,30 +800,31 @@
     gain, inner, last = solve_factors(VISC)
 
     def body(j, carry):
-        m = j // (DROWS // SUB)
-        rows = pl.ds(pl.multiple_of((j % (DROWS // SUB)) * SUB, SUB), SUB)
+        rows = pl.ds(pl.multiple_of(j * SUB, SUB), SUB)
         for src, cnt, shift, dst in ((bu, nx, cx, ou), (bv, ny, cy, ov)):
-            for t in range(I2):
-                cols = slice(LANE * t, LANE * t + LANE)
+            for cols in TILES:
                 n = cnt[rows, cols]
                 run = []
                 for k in range(LEV):
-                    b = src[k, m, rows, cols]
-                    run.append(b if k == I0 else b + gain[k - I1] * run[-I1])
-                nxt = jnp.zeros((SUB, LANE), F32)
-                tot = jnp.zeros((SUB, LANE), F32)
+                    b = [src[k, m, rows, cols] for m in range(MEM)]
+                    run.append(b if k == I0 else [b[m] + gain[k - I1] * run[-I1][m] for m in range(MEM)])
+                nxt = [jnp.zeros((SUB, LANE), F32)] * MEM
+                tot = list(nxt)
                 sol = [None] * LEV
                 for k in range(LEV - I1, -I1, -I1):
-                    coef = last[k] if k == LEV - I1 else jnp.where(n > float(k + I1), inner[k], last[k])
-                    nxt = jnp.where(n > float(k), coef * run[k] + gain[k] * nxt, ZERO)
+                    coef = level_factor(n, k, inner, last)
+                    nxt = [coef * run[k][m] + gain[k] * nxt[m] for m in range(MEM)]
+                    tot = [tot[m] + nxt[m] for m in range(MEM)]
                     sol[k] = nxt
-                    tot = tot + nxt
-                add = shift[m, rows, cols] - tot / jnp.maximum(n, ONE)
+                share = ONE / jnp.maximum(n, ONE)
+                add = [shift[m, rows, cols] - tot[m] * share for m in range(MEM)]
                 for k in range(LEV):
-                    dst[k, m, rows, cols] = jnp.where(n > float(k), sol[k] + add, ZERO)
+                    wet = n > float(k)
+                    for m in range(MEM):
+                        dst[k, m, rows, cols] = jnp.where(wet, sol[k][m] + add[m], ZERO)
         return carry
 
-    lax.fori_loop(I0, MEM * (DROWS // SUB), body, I0)
+    lax.fori_loop(I0, DROWS // SUB, body, I0)
 
 
 def correct_call(bu, bv, nx, ny, cx, cy):

time: 91.7 us -> 88.3 us (0.963)
  Pallas kernels: 90.7 us -> 87.3 us
    pallas_call x1, Pallas kernels: 21.6 us -> 19.2 us  [edges_call(): pl.pallas_call(edges_kernel, name='edges', out_shape=(sds(MEM, ROWS, LANE...]
where the time goes in v3:
time: 88.3 us; the launch traced here: 87.9 us
  Pallas kernels  87.3 us (99%)
    pallas_call x1, Pallas kernels, columns_call(): pl.pallas_call(columns_kernel, name='columns', out_shape=(o3, o3, o3, o3,...  32.8 us
    pallas_call x1, Pallas kernels, edges_call(): pl.pallas_call(edges_kernel, name='edges', out_shape=(sds(MEM, ROWS, LANE...  19.2 us
    pallas_call x1, Pallas kernels, subcycle_call(): pl.pallas_call(subcycle_kernel, name='subcycle', out_shape=(o2,) * 5, in_...  16.4 us
    pallas_call x1, Pallas kernels, correct_call(): pl.pallas_call(correct_kernel, name='correct', grid=(ROWS // DROWS,), out...  10.4 us
    pallas_call x1, Pallas kernels, forcing_call(): pl.pallas_call(forcing_kernel, name='forcing', out_shape=(sds(I2, ROWS, L...  8.42 us

profile of v3, /device:TPU:0, one launch (start us, length us, event | category | flops | bytes accessed | tf_op | source)
XLA Modules:
  0.0 87.9 jit_solution(7369970125741343962)
XLA Ops:
  0.6 19.2 %edges.1 = (f32[2,128,128]{2,1,0:T(8,128)}, f32[2,2,8,128]{3,2,1,0:T(8,128)}, f32[2,2,4,2,16,128]{5,4,3,2,1,0:T(8,128)}, f32[4,128,128]{2,1,0:T(8,128)}, f32[2,4...) custom-call(f32[16,2,128,256]{3,2,1,0:T(8,128)} %u.3, ...), custom_call_target="tpu_custom_call" | custom-call | tf_op jit(solution)/shard_map/edges/pallas_call | solution.py:191
  19.9 32.8 %columns.1 = (f32[16,2,128,256]{3,2,1,0:T(8,128)}, f32[16,2,128,256]{3,2,1,0:T(8,128)}, f32[16,2,128,256]{3,2,1,0:T(8,128)}, f32[16,2,128,256]{3,2,1,0:T(8,128)}...) custom-call(f32[16,2,128,256]{3,2,1,0:T(8,128)} %u.3, ...), custom_call_target="tpu_custom_call" | custom-call | tf_op jit(solution)/shard_map/columns/pallas_call | solution.py:457
  52.7 8.4 %forcing.1 = (f32[2,128,128]{2,1,0:T(8,128)}, f32[2,2,32,128]{3,2,1,0:T(8,128)}, f32[2,2,32,256]{3,2,1,0:T(8,128)}, f32[2,2,32,256]{3,2,1,0:T(8,128)}) custom-call(f32[2,128,256]{2,1,0:T(8,128)} %get-tuple-element.42.sx, f32[2,128,256]{2,1,0:T(8,128)} %get-tuple-element.43.sy), custom_call_target="tpu_custom_call" | custom-call | tf_op jit(solution)/shard_map/forcing/pallas_call | solution.py:509
  61.1 16.4 %subcycle.1 = (f32[2,128,256]{2,1,0:T(8,128)}, f32[2,128,256]{2,1,0:T(8,128)}, f32[2,128,256]{2,1,0:T(8,128)}, f32[2,128,256]{2,1,0:T(8,128)}, f32[2,128,256]{2,1,0:T(8,128)}) custom-call(f32[30]{0:T(128)} %weights.1, f32[2,128,256]{2,1,0:T(8,128)} %eta.3, f32[2,128,256]{2,1,0:T(8,128)} %tx.3, f32[2,128,256]{2,1,0:T(8,128)} %ty.3, ...), custom_call_target="tpu_custom_call" | custom-call | tf_op jit(solution)/shard_map/subcycle/pallas_call | solution.py:777
  77.6 10.4 %correct.1 = (f32[16,2,128,256]{3,2,1,0:T(8,128)}, f32[16,2,128,256]{3,2,1,0:T(8,128)}) custom-call(f32[16,2,128,256]{3,2,1,0:T(8,128)} %get-tuple-element.55.bu, f32[16,2,128,256]{3,2,1,0:T(8,128)} %get-tuple-element.56.bv, f32[128,256]{1,0:T(8,128)} %get-tuple-element.57.nx, f32[128,256]{1,0:T(8,128)} %get-tuple-element.58.ny, ...), custom_call_target="tpu_custom_call" | custom-call | tf_op jit(solution)/shard_map/correct/pallas_call | solution.py:835

commit v4 on v3

--- a/solution.py
+++ b/solution.py
@@ -119,15 +119,15 @@
         sent.append(cp)
         return cp
 
-    for src, dst in ((eta, hre), (tx, hrx), (ty, hry)):
-        send(src.at[:, pl.ds(ROWS - HALO, HALO), :], dst.at[I0], "n")
-        send(src.at[:, pl.ds(I0, HALO), :], dst.at[I1], "s")
-    for src, dst in ((dep, hrh), (kmt, hrk)):
-        send(src.at[pl.ds(ROWS - HALO, HALO), :], dst.at[I0], "n")
-        send(src.at[pl.ds(I0, HALO), :], dst.at[I1], "s")
     lane = lane_ids()
     for cp in loads2:
         cp.wait()
+    for src, dst in ((s2.at[I0], hre), (s2.at[I1], hrx), (s2.at[I2], hry)):
+        send(src.at[:, pl.ds(ROWS - HALO, HALO), :], dst.at[I0], "n")
+        send(src.at[:, pl.ds(I0, HALO), :], dst.at[I1], "s")
+    for src, dst in ((sh, hrh), (sk, hrk)):
+        send(src.at[pl.ds(ROWS - HALO, HALO), :], dst.at[I0], "n")
+        send(src.at[pl.ds(I0, HALO), :], dst.at[I1], "s")
 
     for r in range(ROWS // SUB):
         rows = pl.ds(SUB * r, SUB)
@@ -231,9 +231,6 @@
         rows = pl.ds(pl.multiple_of(CHUNK * c, CHUNK), CHUNK)
         return [pltpu.make_async_copy(a.at[:, :, rows, :], b.at[:, :, rows, :], out_sem.at[i]) for i, (a, b) in enumerate(((obu, bu), (obv, bv), (ost, ot), (oss, os)))]
 
-    for c in range(NCH - I1, NCH - I1 - SLOTS, -I1):
-        for cp in load_copies(jnp.int32(c)):
-            cp.start()
     misc = [
         pltpu.make_async_copy(px, pxs.at[:, pl.ds(SUB, ROWS), :], misc_sem.at[I0]),
         pltpu.make_async_copy(pd.at[I0], pxs.at[:, pl.ds(I0, SUB), :], misc_sem.at[I1]),
@@ -249,6 +246,9 @@
         misc.append(pltpu.make_async_copy(hrk.at[I1, pl.ds(I0, SUB), cols], ki.at[t, pl.ds(SUB + ROWS, SUB), :], misc_sem.at[SUB + 4 * t]))
     for cp in misc:
         cp.start()
+    for c in range(NCH - I1, NCH - I1 - SLOTS, -I1):
+        for cp in load_copies(jnp.int32(c)):
+            cp.start()
     for cp in misc:
         cp.wait()
     lane = lane_ids()
@@ -570,7 +570,7 @@
 SHARED = (I0, I1, I0, I1, I2)
 
 
-def subcycle_kernel(weights, eta, tx, ty, sx, sy, dep, kmt, hx2, hd2, hre, hrx, hry, hrh, hrk, hxs, hds, hrsx, hrsy, eta_out, tx_out, ty_out, cx_out, cy_out, nat, side, hn, kn, e0, e1, t1, t2, f1, f2, hh, kf, gx, gy, gxw, gc, wv, fo, acc1, acc2, ee, ew, tails, sem):
+def subcycle_kernel(weights, eta, tx, ty, sx, sy, dep, kmt, hx2, hd2, hre, hrx, hry, hrh, hrk, hxs, hds, hrsx, hrsy, bu, bv, nx, ny, eta_out, tx_out, ty_out, ou, ov, cx_out, cy_out, sol_u, sol_v, cnt_x, cnt_y, far_sem, nat, side, hn, kn, e0, e1, t1, t2, f1, f2, hh, kf, gx, gy, gxw, gc, wv, fo, acc1, acc2, ee, ew, tails, sem):
     row = lax.axis_index("row")
     not_south = jnp.where(row == I0, ZERO, ONE).astype(F32)
     not_north = jnp.where(row == NR - I1, ZERO, ONE).astype(F32)
@@ -597,6 +597,9 @@
         fetch(rows_.at[I0], dst.at[low, :])
         fetch(rows_.at[I1], dst.at[high, :])
     for cp in copies:
+        cp.start()
+    incoming = [pltpu.make_async_copy(src, dst, far_sem.at[I0]) for src, dst in ((bu, sol_u), (bv, sol_v), (nx, cnt_x), (ny, cnt_y))]
+    for cp in incoming:
         cp.start()
     total = jnp.float32(ZERO)
     moment = jnp.float32(ZERO)
@@ -768,40 +771,13 @@
                 cy_out[m, out_rows, cols] = uy / jnp.where(gyc > ZERO, gyc * (ONE / (WAVE * WAVE)), ONE)
 
     staged(range(base // SUB, top // SUB), end_issue, end_finish, I3)
-
-
-def subcycle_call(weights, *arrays):
-    o2 = sds(MEM, ROWS, COLS)
-    five = pltpu.VMEM((5, BEXT, LANE), F32)
-    three = pltpu.VMEM((I3, BEXT, LANE), F32)
-    return pl.pallas_call(
-        subcycle_kernel,
-        name="subcycle",
-        out_shape=(o2,) * 5,
-        in_specs=[SM] + [ANY] * len(arrays),
-        out_specs=(VM,) * 5,
-        scratch_shapes=[
-            pltpu.VMEM((5, MEM, NEAR, COLS), F32),
-            pltpu.VMEM((6, NEAR, LANE), F32),
-            pltpu.VMEM((NEAR, COLS), F32),
-            pltpu.VMEM((NEAR, COLS), jnp.int32),
-            *[five] * 6, *[three] * 6, *[five] * 4, pltpu.VMEM((I2, 5, BEXT, LANE), F32), pltpu.VMEM((I2, 5, BEXT, LANE), F32),
-            pltpu.SMEM((NSUB,), F32),
-            pltpu.SemaphoreType.DMA,
-        ],
-        compiler_params=pltpu.CompilerParams(vmem_limit_bytes=LIMIT),
-    )(weights, *arrays)
-
-
-DROWS = 16
-
-
-def correct_kernel(bu, bv, nx, ny, cx, cy, ou, ov):
+    for cp in incoming:
+        cp.wait()
     gain, inner, last = solve_factors(VISC)
 
     def body(j, carry):
         rows = pl.ds(pl.multiple_of(j * SUB, SUB), SUB)
-        for src, cnt, shift, dst in ((bu, nx, cx, ou), (bv, ny, cy, ov)):
+        for src, cnt, shift in ((sol_u, cnt_x, cx_out), (sol_v, cnt_y, cy_out)):
             for cols in TILES:
                 n = cnt[rows, cols]
                 run = []
@@ -821,34 +797,58 @@
                 for k in range(LEV):
                     wet = n > float(k)
                     for m in range(MEM):
-                        dst[k, m, rows, cols] = jnp.where(wet, sol[k][m] + add[m], ZERO)
+                        src[k, m, rows, cols] = jnp.where(wet, sol[k][m] + add[m], ZERO)
         return carry
 
-    lax.fori_loop(I0, DROWS // SUB, body, I0)
-
-
-def correct_call(bu, bv, nx, ny, cx, cy):
-    s3 = pl.BlockSpec((LEV, MEM, DROWS, COLS), lambda r: (I0, I0, r, I0))
-    s2 = pl.BlockSpec((MEM, DROWS, COLS), lambda r: (I0, r, I0))
-    s1 = pl.BlockSpec((DROWS, COLS), lambda r: (r, I0))
+    def outgoing(c):
+        rows = pl.ds(HALO * c, HALO)
+        return [pltpu.make_async_copy(a.at[:, :, rows, :], b.at[:, :, rows, :], far_sem.at[I1]) for a, b in ((sol_u, ou), (sol_v, ov))]
+
+    for c in range(ROWS // HALO):
+        lax.fori_loop(c * (HALO // SUB), (c + I1) * (HALO // SUB), body, I0)
+        for cp in outgoing(c):
+            cp.start()
+    for c in range(ROWS // HALO):
+        for cp in outgoing(c):
+            cp.wait()
+
+
+def subcycle_call(weights, *arrays):
+    o2 = sds(MEM, ROWS, COLS)
     o3 = sds(LEV, MEM, ROWS, COLS)
+    five = pltpu.VMEM((5, BEXT, LANE), F32)
+    three = pltpu.VMEM((I3, BEXT, LANE), F32)
     return pl.pallas_call(
-        correct_kernel,
-        name="correct",
-        grid=(ROWS // DROWS,),
-        out_shape=(o3, o3),
-        in_specs=[s3, s3, s1, s1, s2, s2],
-        out_specs=(s3, s3),
+        subcycle_kernel,
+        name="subcycle",
+        out_shape=(o2, o2, o2, o3, o3),
+        in_specs=[SM] + [ANY] * len(arrays),
+        out_specs=(VM, VM, VM, ANY, ANY),
+        scratch_shapes=[
+            pltpu.VMEM((MEM, ROWS, COLS), F32),
+            pltpu.VMEM((MEM, ROWS, COLS), F32),
+            pltpu.VMEM((LEV, MEM, ROWS, COLS), F32),
+            pltpu.VMEM((LEV, MEM, ROWS, COLS), F32),
+            pltpu.VMEM((ROWS, COLS), F32),
+            pltpu.VMEM((ROWS, COLS), F32),
+            pltpu.SemaphoreType.DMA((I2,)),
+            pltpu.VMEM((5, MEM, NEAR, COLS), F32),
+            pltpu.VMEM((6, NEAR, LANE), F32),
+            pltpu.VMEM((NEAR, COLS), F32),
+            pltpu.VMEM((NEAR, COLS), jnp.int32),
+            *[five] * 6, *[three] * 6, *[five] * 4, pltpu.VMEM((I2, 5, BEXT, LANE), F32), pltpu.VMEM((I2, 5, BEXT, LANE), F32),
+            pltpu.SMEM((NSUB,), F32),
+            pltpu.SemaphoreType.DMA,
+        ],
         compiler_params=pltpu.CompilerParams(vmem_limit_bytes=LIMIT),
-    )(bu, bv, nx, ny, cx, cy)
+    )(weights, *arrays)
 
 
 def local_step(u, v, te, sa, eta, tx, ty, dep, kmt, weights):
     px, pd, hr, hx2, hd2, hre, hrx, hry, hrh, hrk = edges_call(u, v, te, sa, eta, tx, ty, dep, kmt)
     bu, bv, ot, os, sx, sy, nx, ny = columns_call(u, v, te, sa, px, pd, hr, dep, kmt, hx2, hrh, hrk)
     hxs, hds, hrsx, hrsy = forcing_call(sx, sy)
-    eta_new, tx_new, ty_new, cx, cy = subcycle_call(weights, eta, tx, ty, sx, sy, dep, kmt, hx2, hd2, hre, hrx, hry, hrh, hrk, hxs, hds, hrsx, hrsy)
-    ou, ov = correct_call(bu, bv, nx, ny, cx, cy)
+    eta_new, tx_new, ty_new, ou, ov = subcycle_call(weights, eta, tx, ty, sx, sy, dep, kmt, hx2, hd2, hre, hrx, hry, hrh, hrk, hxs, hds, hrsx, hrsy, bu, bv, nx, ny)
     return eta_new, tx_new, ty_new, ou, ov, ot, os
 
 

time: 88.3 us -> 86.2 us (0.976)
  Pallas kernels: 87.3 us -> 85.4 us
    pallas_call x2 -> x1, Pallas kernels: 26.8 us -> 23.5 us  [subcycle_call(): pl.pallas_call(subcycle_kernel, name='subcycle', out_shape=(o2, o2, o2, o...]
where the time goes in v4:
time: 86.2 us; the launch traced here: 86.1 us
  Pallas kernels  85.4 us (99%)
    pallas_call x1, Pallas kernels, columns_call(): pl.pallas_call(columns_kernel, name='columns', out_shape=(o3, o3, o3, o3,...  32.7 us
    pallas_call x1, Pallas kernels, subcycle_call(): pl.pallas_call(subcycle_kernel, name='subcycle', out_shape=(o2, o2, o2, o...  23.5 us
    pallas_call x1, Pallas kernels, edges_call(): pl.pallas_call(edges_kernel, name='edges', out_shape=(sds(MEM, ROWS, LANE...  20 us
    pallas_call x1, Pallas kernels, forcing_call(): pl.pallas_call(forcing_kernel, name='forcing', out_shape=(sds(I2, ROWS, L...  9.28 us

profile of v4, /device:TPU:0, one launch (start us, length us, event | category | flops | bytes accessed | tf_op | source)
XLA Modules:
  0.0 86.1 jit_solution(11572543510900792983)
XLA Ops:
  0.6 20.0 %edges.1 = (f32[2,128,128]{2,1,0:T(8,128)}, f32[2,2,8,128]{3,2,1,0:T(8,128)}, f32[2,2,4,2,16,128]{5,4,3,2,1,0:T(8,128)}, f32[4,128,128]{2,1,0:T(8,128)}, f32[2,4...) custom-call(f32[16,2,128,256]{3,2,1,0:T(8,128)} %u.3, ...), custom_call_target="tpu_custom_call" | custom-call | tf_op jit(solution)/shard_map/edges/pallas_call | solution.py:191
  20.6 32.7 %columns.1 = (f32[16,2,128,256]{3,2,1,0:T(8,128)}, f32[16,2,128,256]{3,2,1,0:T(8,128)}, f32[16,2,128,256]{3,2,1,0:T(8,128)}, f32[16,2,128,256]{3,2,1,0:T(8,128)}...) custom-call(f32[16,2,128,256]{3,2,1,0:T(8,128)} %u.3, ...), custom_call_target="tpu_custom_call" | custom-call | tf_op jit(solution)/shard_map/columns/pallas_call | solution.py:457
  53.3 9.3 %forcing.1 = (f32[2,128,128]{2,1,0:T(8,128)}, f32[2,2,32,128]{3,2,1,0:T(8,128)}, f32[2,2,32,256]{3,2,1,0:T(8,128)}, f32[2,2,32,256]{3,2,1,0:T(8,128)}) custom-call(f32[2,128,256]{2,1,0:T(8,128)} %get-tuple-element.40.sx, f32[2,128,256]{2,1,0:T(8,128)} %get-tuple-element.41.sy), custom_call_target="tpu_custom_call" | custom-call | tf_op jit(solution)/shard_map/forcing/pallas_call | solution.py:509
  62.6 23.5 %subcycle.1 = (f32[2,128,256]{2,1,0:T(8,128)}, f32[2,128,256]{2,1,0:T(8,128)}, f32[2,128,256]{2,1,0:T(8,128)}, f32[16,2,128,256]{3,2,1,0:T(8,128)}, f32[16,2,128,256]{3,2,1,0:T(8,128)}) custom-call(f32[30]{0:T(128)} %weights.1, f32[2,128,256]{2,1,0:T(8,128)} %eta.3, f32[2,128,256]{2,1,0:T(8,128)} %tx.3, f32[2,128,256]{2,1,0:T(8,128)} %ty.3, ...), custom_call_target="tpu_custom_call" | custom-call | tf_op jit(solution)/shard_map/subcycle/pallas_call | solution.py:821

commit v5 on v4

--- a/solution.py
+++ b/solution.py
@@ -32,9 +32,9 @@
 BEXT = 208
 NEAR = 192
 F32 = jnp.float32
-CHUNK = 16
+CHUNK = 32
 NCH = ROWS // CHUNK
-SLOTS = I3
+SLOTS = I2
 BPC = CHUNK // SUB
 DEPTH = I2
 MESH = pl.DeviceIdType.MESH
@@ -119,16 +119,15 @@
         sent.append(cp)
         return cp
 
+    for src, dst in ((eta, hre), (tx, hrx), (ty, hry)):
+        send(src.at[:, pl.ds(ROWS - HALO, HALO), :], dst.at[I0], "n")
+        send(src.at[:, pl.ds(I0, HALO), :], dst.at[I1], "s")
+    for src, dst in ((dep, hrh), (kmt, hrk)):
+        send(src.at[pl.ds(ROWS - HALO, HALO), :], dst.at[I0], "n")
+        send(src.at[pl.ds(I0, HALO), :], dst.at[I1], "s")
     lane = lane_ids()
     for cp in loads2:
         cp.wait()
-    for src, dst in ((s2.at[I0], hre), (s2.at[I1], hrx), (s2.at[I2], hry)):
-        send(src.at[:, pl.ds(ROWS - HALO, HALO), :], dst.at[I0], "n")
-        send(src.at[:, pl.ds(I0, HALO), :], dst.at[I1], "s")
-    for src, dst in ((sh, hrh), (sk, hrk)):
-        send(src.at[pl.ds(ROWS - HALO, HALO), :], dst.at[I0], "n")
-        send(src.at[pl.ds(I0, HALO), :], dst.at[I1], "s")
-
     for r in range(ROWS // SUB):
         rows = pl.ds(SUB * r, SUB)
         for i in range(I3):

time: 86.2 us -> 86.4 us (level)
    pallas_call x1, Pallas kernels: 32.7 us -> 34.5 us  [columns_call(): pl.pallas_call(columns_kernel, name='columns', out_shape=(o3, o3, o3, o3,...]
    pallas_call x1, Pallas kernels: 9.28 us -> 8.42 us  [forcing_call(): pl.pallas_call(forcing_kernel, name='forcing', out_shape=(sds(I2, ROWS, L...]
where the time goes in v5:
time: 86.4 us; the launch traced here: 86.3 us
  Pallas kernels  85.7 us (99%)
    pallas_call x1, Pallas kernels, columns_call(): pl.pallas_call(columns_kernel, name='columns', out_shape=(o3, o3, o3, o3,...  34.5 us
    pallas_call x1, Pallas kernels, subcycle_call(): pl.pallas_call(subcycle_kernel, name='subcycle', out_shape=(o2, o2, o2, o...  23.5 us
    pallas_call x1, Pallas kernels, edges_call(): pl.pallas_call(edges_kernel, name='edges', out_shape=(sds(MEM, ROWS, LANE...  19.2 us
    pallas_call x1, Pallas kernels, forcing_call(): pl.pallas_call(forcing_kernel, name='forcing', out_shape=(sds(I2, ROWS, L...  8.42 us

profile of v5, /device:TPU:0, one launch (start us, length us, event | category | flops | bytes accessed | tf_op | source)
XLA Modules:
  0.0 86.3 jit_solution(129848101531758984)
XLA Ops:
  0.6 19.2 %edges.1 = (f32[2,128,128]{2,1,0:T(8,128)}, f32[2,2,8,128]{3,2,1,0:T(8,128)}, f32[2,2,4,2,16,128]{5,4,3,2,1,0:T(8,128)}, f32[4,128,128]{2,1,0:T(8,128)}, f32[2,4...) custom-call(f32[16,2,128,256]{3,2,1,0:T(8,128)} %u.3, ...), custom_call_target="tpu_custom_call" | custom-call | tf_op jit(solution)/shard_map/edges/pallas_call | solution.py:190
  19.9 34.5 %columns.1 = (f32[16,2,128,256]{3,2,1,0:T(8,128)}, f32[16,2,128,256]{3,2,1,0:T(8,128)}, f32[16,2,128,256]{3,2,1,0:T(8,128)}, f32[16,2,128,256]{3,2,1,0:T(8,128)}...) custom-call(f32[16,2,128,256]{3,2,1,0:T(8,128)} %u.3, ...), custom_call_target="tpu_custom_call" | custom-call | tf_op jit(solution)/shard_map/columns/pallas_call | solution.py:456
  54.4 8.4 %forcing.1 = (f32[2,128,128]{2,1,0:T(8,128)}, f32[2,2,32,128]{3,2,1,0:T(8,128)}, f32[2,2,32,256]{3,2,1,0:T(8,128)}, f32[2,2,32,256]{3,2,1,0:T(8,128)}) custom-call(f32[2,128,256]{2,1,0:T(8,128)} %get-tuple-element.40.sx, f32[2,128,256]{2,1,0:T(8,128)} %get-tuple-element.41.sy), custom_call_target="tpu_custom_call" | custom-call | tf_op jit(solution)/shard_map/forcing/pallas_call | solution.py:508
  62.9 23.5 %subcycle.1 = (f32[2,128,256]{2,1,0:T(8,128)}, f32[2,128,256]{2,1,0:T(8,128)}, f32[2,128,256]{2,1,0:T(8,128)}, f32[16,2,128,256]{3,2,1,0:T(8,128)}, f32[16,2,128,256]{3,2,1,0:T(8,128)}) custom-call(f32[30]{0:T(128)} %weights.1, f32[2,128,256]{2,1,0:T(8,128)} %eta.3, f32[2,128,256]{2,1,0:T(8,128)} %tx.3, f32[2,128,256]{2,1,0:T(8,128)} %ty.3, ...), custom_call_target="tpu_custom_call" | custom-call | tf_op jit(solution)/shard_map/subcycle/pallas_call | solution.py:820

commit v6 on v5

--- a/solution.py
+++ b/solution.py
@@ -32,9 +32,9 @@
 BEXT = 208
 NEAR = 192
 F32 = jnp.float32
-CHUNK = 32
+CHUNK = 16
 NCH = ROWS // CHUNK
-SLOTS = I2
+SLOTS = I3
 BPC = CHUNK // SUB
 DEPTH = I2
 MESH = pl.DeviceIdType.MESH

time: 86.4 us -> 84.6 us (0.979)
  Pallas kernels: 85.7 us -> 83.8 us
    pallas_call x1, Pallas kernels: 34.5 us -> 32.7 us  [columns_call(): pl.pallas_call(columns_kernel, name='columns', out_shape=(o3, o3, o3, o3,...]
where the time goes in v6:
time: 84.6 us; the launch traced here: 84.5 us
  Pallas kernels  83.8 us (99%)
    pallas_call x1, Pallas kernels, columns_call(): pl.pallas_call(columns_kernel, name='columns', out_shape=(o3, o3, o3, o3,...  32.7 us
    pallas_call x1, Pallas kernels, subcycle_call(): pl.pallas_call(subcycle_kernel, name='subcycle', out_shape=(o2, o2, o2, o...  23.5 us
    pallas_call x1, Pallas kernels, edges_call(): pl.pallas_call(edges_kernel, name='edges', out_shape=(sds(MEM, ROWS, LANE...  19.2 us
    pallas_call x1, Pallas kernels, forcing_call(): pl.pallas_call(forcing_kernel, name='forcing', out_shape=(sds(I2, ROWS, L...  8.42 us

profile of v6, /device:TPU:0, one launch (start us, length us, event | category | flops | bytes accessed | tf_op | source)
XLA Modules:
  0.0 84.5 jit_solution(12732869606057495780)
XLA Ops:
  0.6 19.2 %edges.1 = (f32[2,128,128]{2,1,0:T(8,128)}, f32[2,2,8,128]{3,2,1,0:T(8,128)}, f32[2,2,4,2,16,128]{5,4,3,2,1,0:T(8,128)}, f32[4,128,128]{2,1,0:T(8,128)}, f32[2,4...) custom-call(f32[16,2,128,256]{3,2,1,0:T(8,128)} %u.3, ...), custom_call_target="tpu_custom_call" | custom-call | tf_op jit(solution)/shard_map/edges/pallas_call | solution.py:190
  19.9 32.7 %columns.1 = (f32[16,2,128,256]{3,2,1,0:T(8,128)}, f32[16,2,128,256]{3,2,1,0:T(8,128)}, f32[16,2,128,256]{3,2,1,0:T(8,128)}, f32[16,2,128,256]{3,2,1,0:T(8,128)}...) custom-call(f32[16,2,128,256]{3,2,1,0:T(8,128)} %u.3, ...), custom_call_target="tpu_custom_call" | custom-call | tf_op jit(solution)/shard_map/columns/pallas_call | solution.py:456
  52.6 8.4 %forcing.1 = (f32[2,128,128]{2,1,0:T(8,128)}, f32[2,2,32,128]{3,2,1,0:T(8,128)}, f32[2,2,32,256]{3,2,1,0:T(8,128)}, f32[2,2,32,256]{3,2,1,0:T(8,128)}) custom-call(f32[2,128,256]{2,1,0:T(8,128)} %get-tuple-element.40.sx, f32[2,128,256]{2,1,0:T(8,128)} %get-tuple-element.41.sy), custom_call_target="tpu_custom_call" | custom-call | tf_op jit(solution)/shard_map/forcing/pallas_call | solution.py:508
  61.0 23.5 %subcycle.1 = (f32[2,128,256]{2,1,0:T(8,128)}, f32[2,128,256]{2,1,0:T(8,128)}, f32[2,128,256]{2,1,0:T(8,128)}, f32[16,2,128,256]{3,2,1,0:T(8,128)}, f32[16,2,128,256]{3,2,1,0:T(8,128)}) custom-call(f32[30]{0:T(128)} %weights.1, f32[2,128,256]{2,1,0:T(8,128)} %eta.3, f32[2,128,256]{2,1,0:T(8,128)} %tx.3, f32[2,128,256]{2,1,0:T(8,128)} %ty.3, ...), custom_call_target="tpu_custom_call" | custom-call | tf_op jit(solution)/shard_map/subcycle/pallas_call | solution.py:820
